TPU v7x, 32 devices: a whole 2x2x4 slice. The times are simulated.
32 devices in a mesh: tm: 8 (over z, y), space: 4 (over x, core).
Axes of the slice: x: 2, y: 2, z: 4, core: 2. Of those that a mesh axis runs over, the one named last changes fastest.
Arguments:
- starts: float32 [8, 5, 16, 64, 128], P('tm', None, 'space'), may hold values from -4 to 4
- source: float32 [5, 16, 64, 128], P(None, 'space'), may hold values from -4 to 4
Outputs:
- ends: float32 [8, 5, 16, 64, 128], P('tm', None, 'space')
- slice_norms: float32 [8], P('tm')
- total_norm: float32 [1], replicated
All inputs are finite; a program needn't handle non-finite values.
Results may differ from a plain program's by a relative error of at most 0.0003.
Values sent between devices are 32-bit elements; how exact they have to be, the bound alone decides.
A program may use at most 64 MiB of HBM per device.

v0:
```python
import functools
import math

import jax
import jax.numpy as jnp
import numpy as np
from jax import lax
from jax.experimental import pallas as pl
from jax.experimental.pallas import tpu as pltpu
from jax.sharding import PartitionSpec as P

viscosity = 0.08
diffusivity = 0.05
compress_rate = 0.25
time_step = 0.5
diffusion_number = 0.08
advect_xaxis = 0.2
advect_yaxis = 0.15
advect_zaxis = 0.1
epsilon = 1e-06
MESH = pl.DeviceIdType.MESH
PAD = 8
CHUNK = 16
LANES = 128


def tables(depth, rows, cols, spaces, steps):
    keep_y, keep_x = rows // 8, cols // 16
    slot = 2 * keep_x
    per = LANES // (slot * depth)
    full = depth * spaces
    k = np.arange(keep_x)
    x = np.arange(cols)
    ax = 2 * math.pi / cols * ((x[:, None] * k[None, :]) % cols)
    weight = np.where(k == 0, 1.0, 2.0) / (full * rows * cols)
    xf = np.zeros((2 * cols, LANES))
    xi = np.zeros((LANES, 2 * cols))
    for i in range(2):
        at = i * slot
        xf[i * cols : (i + 1) * cols, at : at + keep_x] = np.cos(ax)
        xf[i * cols : (i + 1) * cols, at + keep_x : at + slot] = -np.sin(ax)
        xi[at : at + keep_x, i * cols : (i + 1) * cols] = (np.cos(ax) * weight).T
        xi[at + keep_x : at + slot, i * cols : (i + 1) * cols] = (-np.sin(ax) * weight).T
    ky = np.arange(2 * keep_y)
    ky = np.where(ky < keep_y, ky, ky - 2 * keep_y)
    y = np.arange(rows)
    ay = 2 * math.pi / rows * ((ky[:, None] * y[None, :]) % rows)
    yf = np.concatenate([np.cos(ay), np.sin(ay)], axis=1)
    yi = np.concatenate([np.cos(ay).T, -np.sin(ay).T], axis=1)
    kz = np.arange(full)
    width = full * keep_x
    half = depth * slot
    zf = np.zeros((LANES, per * 2 * width))
    for fp in range(per):
        for z in range(depth):
            a = 2 * math.pi / full * ((kz * z) % full)
            for kk in range(keep_x):
                row = fp * half + z * slot + kk
                re = fp * 2 * width + kz * keep_x + kk
                im = re + width
                zf[row, re] = np.cos(a)
                zf[row, im] = -np.sin(a)
                zf[row + keep_x, re] = np.sin(a)
                zf[row + keep_x, im] = np.cos(a)
    zi = np.zeros((2 * width, full * slot))
    for z in range(full):
        a = 2 * math.pi / full * ((kz * z) % full)
        for kk in range(keep_x):
            re = kz * keep_x + kk
            im = re + width
            col = z * slot + kk
            zi[re, col] = np.cos(a)
            zi[im, col] = -np.sin(a)
            zi[re, col + keep_x] = np.sin(a)
            zi[im, col + keep_x] = np.cos(a)
    tz = 2 * math.pi / full * kz
    ty = 2 * math.pi / rows * ky
    tx = 2 * math.pi / cols * k
    live = (ky != -keep_y).astype(np.float64)[:, None, None]
    real = 1.0 + diffusion_number * (
        (2 * np.cos(ty) - 2)[:, None, None]
        + (2 * np.cos(tz) - 2)[None, :, None]
        + (2 * np.cos(tx) - 2)[None, None, :]
    )
    imag = -(
        advect_yaxis * np.sin(ty)[:, None, None]
        + advect_zaxis * np.sin(tz)[None, :, None]
        + advect_xaxis * np.sin(tx)[None, None, :]
    )
    symbol = (real + 1j * imag) * live
    powers = np.stack([symbol**p for p in range(1, max(steps, 2))])
    powers = np.stack([powers.real, powers.imag], axis=1).reshape(-1, 2, 2 * keep_y, width)
    return [xf, yf, zf, zi, yi, xi], powers.astype(np.float32)


def halves(table):
    high = table.astype(jnp.bfloat16)
    low = (table - high.astype(np.float64)).astype(jnp.bfloat16)
    return np.stack([high, low])


def split(values):
    high = values.astype(jnp.bfloat16)
    return high, (values - high.astype(jnp.float32)).astype(jnp.bfloat16)


def dot(a, b):
    return jnp.dot(a, b, preferred_element_type=jnp.float32)


def times(values, table):
    high, low = split(values)
    return dot(high, table[0]) + dot(low, table[0]) + dot(high, table[1])


def under(table, values):
    high, low = split(values)
    return dot(table[0], high) + dot(table[0], low) + dot(table[1], high)


def kernel(
    sizes, starts, source, xf_h, yf_h, zf_h, zi_h, yi_h, xi_h, sym_h,
    fine_out, fix_out, slice_out, total_out,
    y1, y2, y3, y4, src, fine, fixes, halo, xf, yf, zf, zi, yi, xi, sym,
    own, jumps, ahead, mode_send, mode_recv, square_send, squares,
    load_sem, table_sem, halo_send, halo_recv, ahead_sems, jump_send, jump_recv,
    mode_ssem, mode_rsem, sq_send, sq_recv, out_sem, relays,
):
    times_n, spaces, fields, depth, rows, cols = sizes
    keep_y, keep_x = rows // 8, cols // 16
    slot = 2 * keep_x
    ky = 2 * keep_y
    layers = fields * depth
    slots = LANES // slot
    groups = -(-layers // slots)
    per = LANES // (slot * depth)
    chunks = rows // CHUNK
    n = lax.axis_index("tm")
    s = lax.axis_index("space")
    me = n * spaces + s
    up = lax.rem(s + 1, spaces)
    down = lax.rem(s + spaces - 1, spaces)

    barrier = pltpu.get_barrier_semaphore()

    def near(distance, act):
        for side, target in enumerate((n - distance, n + distance)):
            pl.when((target >= 0) & (target < times_n))(functools.partial(act, side, target))

    def enter(target, where):
        pl.semaphore_signal(barrier, inc=1, device_id=(target, where), device_id_type=MESH)

    for offset in range(1, spaces):
        enter(n, lax.rem(s + offset, spaces))
    near(1, lambda side, target: enter(target, s))
    loads = [
        pltpu.make_async_copy(starts.at[0, :, 0], y1.at[:, 0, pl.ds(PAD, rows)], load_sem.at[0]),
        pltpu.make_async_copy(
            starts.at[0, :, depth - 1], y1.at[:, depth - 1, pl.ds(PAD, rows)], load_sem.at[4]
        ),
        pltpu.make_async_copy(
            starts.at[0, :, pl.ds(1, depth - 2)],
            y1.at[:, pl.ds(1, depth - 2), pl.ds(PAD, rows)],
            load_sem.at[5],
        ),
        pltpu.make_async_copy(
            starts.at[0, :, :, pl.ds(rows - PAD, PAD)], y1.at[:, :, pl.ds(0, PAD)], load_sem.at[1]
        ),
        pltpu.make_async_copy(
            starts.at[0, :, :, pl.ds(0, PAD)], y1.at[:, :, pl.ds(PAD + rows, PAD)], load_sem.at[2]
        ),
        pltpu.make_async_copy(source, src, load_sem.at[3]),
    ]
    for copy in loads:
        copy.start()
    fills = [
        pltpu.make_async_copy(a, b, table_sem.at[i])
        for i, (a, b) in enumerate(
            [(xf_h, xf), (yf_h, yf), (zf_h, zf), (zi_h, zi), (yi_h, yi), (xi_h, xi), (sym_h, sym)]
        )
    ]
    for copy in fills:
        copy.start()
    for copy in loads[:2]:
        copy.wait()
    beside = jnp.where(n > 0, 1, 0) + jnp.where(n < times_n - 1, 1, 0)
    pl.semaphore_wait(barrier, spaces - 1 + beside)

    def relay(level):
        near(
            2**level,
            lambda side, target: pl.semaphore_signal(
                relays.at[level, side], inc=1, device_id=(target, s), device_id_type=MESH
            ),
        )

    def heard(level):
        near(2**level, lambda side, target: pl.semaphore_wait(relays.at[level, 1 - side], 1))

    levels = (times_n - 1).bit_length()

    states = [y1, y2, y3, y4]

    def halo_copy(stage, side, chunk):
        r0 = pl.multiple_of(chunk * CHUNK, CHUNK)
        state = states[stage]
        layer = depth - 1 if side == 0 else 0
        return pltpu.make_async_remote_copy(
            src_ref=state.at[:, layer, pl.ds(pl.multiple_of(PAD + r0, 8), CHUNK)],
            dst_ref=halo.at[stage, side, :, pl.ds(r0, CHUNK)],
            send_sem=halo_send.at[stage, side, chunk],
            recv_sem=halo_recv.at[stage, side, chunk],
            device_id=(n, up if side == 0 else down),
            device_id_type=MESH,
        )

    def send_first(c, carry):
        for side in range(2):
            halo_copy(0, side, c).start()
        return carry

    lax.fori_loop(0, chunks, send_first, 0)
    relay(0)

    lane = lax.broadcasted_iota(jnp.int32, (1, LANES), 1)
    first = lax.rem(lane, slot) < keep_x

    def swapped(values):
        return jnp.where(
            first, pltpu.roll(values, LANES - keep_x, 1), -pltpu.roll(values, keep_x, 1)
        )

    def transform(layer_of):
        pairs = jnp.concatenate(
            [
                jnp.concatenate([layer_of(2 * p), layer_of(2 * p + 1)], axis=1)
                for p in range(layers // 2)
            ],
            axis=0,
        )
        packed = times(pairs, xf)
        result = []
        for g in range(groups):
            total = None
            for p in range(slots // 2):
                index = g * (slots // 2) + p
                if index < layers // 2:
                    piece = packed[index * rows : (index + 1) * rows]
                    if p > 0:
                        piece = pltpu.roll(piece, 2 * p * slot, 1)
                    total = piece if total is None else total + piece
            result.append(total)
        both = [jnp.concatenate([t, swapped(t)], axis=0) for t in result]
        spec = under(yf, jnp.concatenate(both, axis=1))
        return jnp.concatenate([spec[:, g * LANES : (g + 1) * LANES] for g in range(groups)], axis=0)

    for copy in loads[2:] + fills:
        copy.wait()

    own[...] = transform(lambda l: y1[l // depth, l % depth, pl.ds(PAD, rows)])
    ahead_copy = pltpu.make_async_remote_copy(
        src_ref=own,
        dst_ref=ahead,
        send_sem=ahead_sems.at[0],
        recv_sem=ahead_sems.at[1],
        device_id=(jnp.maximum(n - 1, 0), s),
        device_id_type=MESH,
    )

    @pl.when(n > 0)
    def _():
        ahead_copy.start()

    def update(stage, z, r0, below, above):
        state = states[stage]
        mid, xm, xp, ym, yp = [], [], [], [], []
        rolled = CHUNK + 2 * PAD
        for f in range(fields):
            wide = state[f, z, pl.ds(r0, rolled)]
            centre = wide[PAD : PAD + CHUNK]
            mid.append(centre)
            ym.append(pltpu.roll(wide, 1, 0)[PAD : PAD + CHUNK])
            yp.append(pltpu.roll(wide, rolled - 1, 0)[PAD : PAD + CHUNK])
            xm.append(pltpu.roll(centre, 1, 1))
            xp.append(pltpu.roll(centre, cols - 1, 1))
        zm = [below(f) for f in range(fields)]
        zp = [above(f) for f in range(fields)]
        sides = [xm, xp, ym, yp, zm, zp]
        factors = []
        for axis, speed in enumerate((advect_xaxis, advect_yaxis, advect_zaxis)):
            factors.append((viscosity + 0.5 * speed) + 0.5 * sides[2 * axis][axis])
            factors.append((viscosity - 0.5 * speed) - 0.5 * sides[2 * axis + 1][axis])
        shift = viscosity - diffusivity
        rates = []
        for f in range(fields):
            forcing = src[f, z, pl.ds(r0, CHUNK)]
            if f == 3:
                total = (
                    (xp[0] - xm[0]) + (yp[1] - ym[1]) + (zp[2] - zm[2])
                ) * (-0.5 * compress_rate)
            else:
                gain = viscosity if f < 3 else diffusivity
                total = (-6.0 * gain) * mid[f]
                for factor, side in zip(factors, sides):
                    total = total + (factor if f < 3 else factor - shift) * side[f]
                if f < 3:
                    total = total + 0.5 * (sides[2 * f][3] - sides[2 * f + 1][3])
            rates.append(total + forcing)
        share = time_step / 6.0 * (1.0, 2.0, 2.0, 1.0)[stage]
        for f in range(fields):
            at = f * depth + z
            here = pl.ds(r0, CHUNK)
            begin = y1[f, z, pl.ds(pl.multiple_of(r0 + PAD, 8), CHUNK)]
            done = begin if stage == 0 else fine[at, here]
            fine[at, here] = done + share * rates[f]
            if stage < 3:
                later = states[stage + 1]
                step = (0.5, 0.5, 1.0)[stage] * time_step
                value = begin + step * rates[f]
                later[f, z, pl.ds(pl.multiple_of(r0 + PAD, 8), CHUNK)] = value

                @pl.when(r0 == 0)
                def _():
                    later[f, z, pl.ds(PAD + rows, PAD)] = value[:PAD]

                @pl.when(r0 == rows - CHUNK)
                def _():
                    later[f, z, pl.ds(0, PAD)] = value[CHUNK - PAD :]

    for stage in range(4):
        state = states[stage]

        def inner(i, carry):
            z = 1 + i // chunks
            r0 = pl.multiple_of(lax.rem(i, chunks) * CHUNK, CHUNK)
            at = pl.ds(pl.multiple_of(r0 + PAD, 8), CHUNK)
            update(stage, z, r0, lambda f: state[f, z - 1, at], lambda f: state[f, z + 1, at])
            return carry

        def edge(c, carry):
            r0 = pl.multiple_of(c * CHUNK, CHUNK)
            at = pl.ds(pl.multiple_of(r0 + PAD, 8), CHUNK)
            for side in range(2):
                halo_copy(stage, side, c).wait_recv()
                here = lambda f: halo[stage, side, f, pl.ds(r0, CHUNK)]
                if side == 0:
                    update(stage, 0, r0, here, lambda f: state[f, 1, at])
                else:
                    update(stage, depth - 1, r0, lambda f: state[f, depth - 2, at], here)
                if stage < 3:
                    halo_copy(stage + 1, 1 - side, c).start()
            return carry

        lax.fori_loop(0, (depth - 2) * chunks, inner, 0)
        lax.fori_loop(0, chunks, edge, 0)
        for level in range(levels):
            if min(level, 2) == stage:
                heard(level)
                if level + 1 < levels:
                    relay(level + 1)

    outs = [pltpu.make_async_copy(fine, fine_out, out_sem.at[0])]
    outs[0].start()
    spec = transform(lambda l: fine[l])

    @pl.when(n < times_n - 1)
    def _():
        ahead_copy.wait_recv()
        jumps[n] = spec - ahead[...]

    def jump_copy(slot_id, sem_id, target):
        return pltpu.make_async_remote_copy(
            src_ref=jumps.at[slot_id],
            dst_ref=jumps.at[slot_id],
            send_sem=jump_send.at[sem_id],
            recv_sem=jump_recv.at[slot_id],
            device_id=(target, s),
            device_id_type=MESH,
        )

    def send_jump(i, carry):
        target = times_n - 1 - i
        jump_copy(n, target, target).start()
        return carry

    lax.fori_loop(0, times_n - 1 - n, send_jump, 0)

    width = depth * spaces * keep_x

    def collect(i, carry):
        m = n - 1 - i
        jump_copy(m, m, n).wait_recv()
        fresh = times(jumps[m], zf)
        gain_re = jnp.concatenate([sym[i, 0]] * groups, axis=0)
        gain_im = jnp.concatenate([sym[i, 1]] * groups, axis=0)
        result = []
        for p in range(per):
            re = fresh[:, 2 * p * width : (2 * p + 1) * width]
            im = fresh[:, (2 * p + 1) * width : (2 * p + 2) * width]
            result.append(carry[2 * p] + (gain_re * re - gain_im * im))
            result.append(carry[2 * p + 1] + (gain_re * im + gain_im * re))
        return tuple(result)

    zero = jnp.zeros((groups * ky, width), jnp.float32)
    carry = lax.fori_loop(0, n, collect, (zero,) * (2 * per))
    stacked = jnp.concatenate(
        [jnp.concatenate([carry[2 * p], carry[2 * p + 1]], axis=1) for p in range(per)], axis=0
    )
    back = times(stacked, zi)
    half = depth * slot
    height = groups * ky

    def piece(offset):
        total = None
        at = offset * half
        tile, inside = at // LANES * LANES, at % LANES
        part = lax.broadcasted_iota(jnp.int32, (1, LANES), 1) // half
        for p in range(per):
            block = back[p * height : (p + 1) * height, tile : tile + LANES]
            move = (p * half - inside) % LANES
            if move:
                block = pltpu.roll(block, move, 1)
            total = block if total is None else jnp.where(part == p, block, total)
        return total

    def mode_copy(offset):
        return pltpu.make_async_remote_copy(
            src_ref=mode_send.at[offset - 1],
            dst_ref=mode_recv.at[offset - 1],
            send_sem=mode_ssem.at[offset - 1],
            recv_sem=mode_rsem.at[offset - 1],
            device_id=(n, lax.rem(s + offset, spaces)),
            device_id_type=MESH,
        )

    for offset in range(1, spaces):
        mode_send[offset - 1] = piece(offset)
        mode_copy(offset).start()
    modes = piece(0)
    for offset in range(1, spaces):
        mode_copy(offset).wait_recv()
        modes = modes + mode_recv[offset - 1]

    weight = jnp.where(lax.rem(lane, keep_x) == 0, 1.0, 2.0)
    scaled = modes * (1.0 / (depth * spaces * rows * cols))
    square = jnp.sum(
        jnp.sum(scaled * scaled * weight, axis=0, keepdims=True), axis=1, keepdims=True
    ) * float(rows * cols)
    square_send[...] = jnp.broadcast_to(square, (1, LANES))
    squares[me] = jnp.broadcast_to(square, (1, LANES))

    def square_copy(index, sem_id, target):
        return pltpu.make_async_remote_copy(
            src_ref=square_send,
            dst_ref=squares.at[index],
            send_sem=sq_send.at[sem_id],
            recv_sem=sq_recv.at[index],
            device_id=target,
            device_id_type=MESH,
        )

    def others(act):
        def body(dt, carry):
            t = n - dt
            t = jnp.where(t < 0, t + times_n, t)
            for ds in range(spaces):
                where = s + ds
                where = jnp.where(where >= spaces, where - spaces, where)
                run = functools.partial(act, dt * spaces + ds, t, where)
                if ds == 0:
                    pl.when(dt > 0)(run)
                else:
                    run()
            return carry

        if times_n <= 8:
            for dt in range(times_n):
                body(dt, 0)
        else:
            lax.fori_loop(0, times_n, body, 0)

    others(lambda k, t, where: square_copy(me, k, (t, where)).start())

    both = [
        jnp.concatenate([t, swapped(t)], axis=0)
        for t in (modes[g * ky : (g + 1) * ky] for g in range(groups))
    ]
    planes = under(yi, jnp.concatenate(both, axis=1))
    for g in range(groups):
        plane = planes[:, g * LANES : (g + 1) * LANES]
        count = min(slots, layers - g * slots) // 2
        shifted = [
            plane if p == 0 else pltpu.roll(plane, LANES - 2 * p * slot, 1) for p in range(count)
        ]
        fix = times(jnp.concatenate(shifted, axis=0), xi)
        for p in range(count):
            for i in range(2):
                l = g * slots + 2 * p + i
                fixes[l] = fix[p * rows : (p + 1) * rows, i * cols : (i + 1) * cols]
        held = pl.ds(g * slots, 2 * count)
        copy = pltpu.make_async_copy(fixes.at[held], fix_out.at[held], out_sem.at[1 + g])
        copy.start()
        outs.append(copy)

    others(
        lambda k, t, where: square_copy(t * spaces + where, k, (t, where)).wait_recv()
    )
    cells = fields * depth * spaces * rows * cols
    mine = jnp.sum(squares[pl.ds(n * spaces, spaces)], axis=0)
    every = jnp.sum(squares[...], axis=0)
    slice_out[0] = jnp.sqrt(mine * (1.0 / cells) + epsilon)[0, 0]
    total_out[0] = jnp.sqrt(every * (1.0 / (cells * times_n)) + epsilon)[0, 0]

    others(lambda k, t, where: square_copy(me, k, (t, where)).wait_send())

    def drain_jump(i, carry):
        target = times_n - 1 - i
        jump_copy(n, target, target).wait_send()
        return carry

    lax.fori_loop(0, times_n - 1 - n, drain_jump, 0)

    @pl.when(n > 0)
    def _():
        ahead_copy.wait_send()

    for stage in range(4):

        def drain_halo(c, carry):
            for side in range(2):
                halo_copy(stage, side, c).wait_send()
            return carry

        lax.fori_loop(0, chunks, drain_halo, 0)
    for offset in range(1, spaces):
        mode_copy(offset).wait_send()
    for copy in outs:
        copy.wait()


def solution(mesh):
    times_n, spaces = mesh.shape["tm"], mesh.shape["space"]

    def step(starts, source):
        _, fields, depth, rows, cols = starts.shape
        keep_y, keep_x = rows // 8, cols // 16
        matrices, symbol = tables(depth, rows, cols, spaces, times_n)
        constants = [halves(t) for t in matrices] + [symbol]
        ky, slot = 2 * keep_y, 2 * keep_x
        groups = -(-fields * depth // (LANES // slot))
        height = groups * ky
        chunks = rows // CHUNK
        devices = times_n * spaces
        state = pltpu.VMEM((fields, depth, rows + 2 * PAD, cols), jnp.float32)
        dma = pltpu.SemaphoreType.DMA
        layer_shape = (fields * depth, rows, cols)
        fine, fix, slice_norm, total_norm = pl.pallas_call(
            functools.partial(kernel, (times_n, spaces, fields, depth, rows, cols)),
            out_shape=(
                jax.ShapeDtypeStruct(layer_shape, jnp.float32),
                jax.ShapeDtypeStruct(layer_shape, jnp.float32),
                jax.ShapeDtypeStruct((1,), jnp.float32),
                jax.ShapeDtypeStruct((1,), jnp.float32),
            ),
            in_specs=[pl.BlockSpec(memory_space=pltpu.HBM)] * (2 + len(constants)),
            out_specs=(
                pl.BlockSpec(memory_space=pl.ANY),
                pl.BlockSpec(memory_space=pl.ANY),
                pl.BlockSpec(memory_space=pltpu.SMEM),
                pl.BlockSpec(memory_space=pltpu.SMEM),
            ),
            scratch_shapes=[
                state, state, state, state,
                pltpu.VMEM((fields, depth, rows, cols), jnp.float32),
                pltpu.VMEM(layer_shape, jnp.float32),
                pltpu.VMEM(layer_shape, jnp.float32),
                pltpu.VMEM((4, 2, fields, rows, cols), jnp.float32),
                *[pltpu.VMEM(c.shape, c.dtype) for c in constants],
                pltpu.VMEM((height, LANES), jnp.float32),
                pltpu.VMEM((times_n, height, LANES), jnp.float32),
                pltpu.VMEM((height, LANES), jnp.float32),
                pltpu.VMEM((spaces - 1, height, LANES), jnp.float32),
                pltpu.VMEM((spaces - 1, height, LANES), jnp.float32),
                pltpu.VMEM((1, LANES), jnp.float32),
                pltpu.VMEM((devices, 1, LANES), jnp.float32),
                dma((6,)), dma((len(constants),)),
                dma((4, 2, chunks)), dma((4, 2, chunks)), dma((2,)),
                dma((times_n,)), dma((times_n,)),
                dma((spaces - 1,)), dma((spaces - 1,)),
                dma((devices,)), dma((devices,)), dma((2 * fields,)),
                pltpu.SemaphoreType.REGULAR(((times_n - 1).bit_length(), 2)),
            ],
            compiler_params=pltpu.CompilerParams(
                collective_id=0, has_side_effects=True, vmem_limit_bytes=67043328
            ),
        )(starts, source, *[jnp.asarray(c) for c in constants])
        return (fine + fix).reshape(starts.shape), slice_norm, total_norm

    return jax.shard_map(
        step,
        mesh=mesh,
        in_specs=(P("tm", None, "space", None, None), P(None, "space", None, None)),
        out_specs=(P("tm", None, "space", None, None), P("tm"), P()),
        check_vma=False,
    )
```

profile of v0, /device:TPU:0, one launch (start us, length us, event | category | flops | bytes accessed | tf_op | source)
XLA Modules:
  0.0 43.9 jit_solution(709130385524806727)
XLA Ops:
  0.6 37.5 %shard_map.112 = (f32[20,64,128]{2,1,0:T(8,128)}, f32[20,64,128]{2,1,0:T(8,128)}, f32[1]{0:T(128)}, f32[1]{0:T(128)}) custom-call(f32[1,5,4,64,128]{4,3,2,1,0:T(8,128)} %starts.1, f32[5,4,64,128]{3,2,1,0:T(8,128)} %source.1, bf16[2,256,128]{2,1,0:T(8,128)(2,1)} %constant.14.clone.xf_h, bf16[2,16,128]{2,1,0:T(8,128)(2,1)} %constant.15.clone.yf_h, ...), custom_call_target="tpu_custom_call" | custom-call | tf_op jit(solution)/shard_map/pallas_call | solution.py:557
  38.2 2.2 %add.3 = f32[20,64,128]{2,1,0:T(8,128)} add(f32[20,64,128]{2,1,0:T(8,128)} %get-tuple-element.7, f32[20,64,128]{2,1,0:T(8,128)} %get-tuple-element.8) | non-fusion elementwise | flops 163840 | bytes 1966080 | tf_op jit(solution)/shard_map/add | solution.py:597
where the time goes:
time: 44.1 us; the launch traced here: 43.9 us
  Pallas kernels  37.5 us (85%)
  between operations  4.2 us (10%)
  other arithmetic  2.21 us (5%)
    pallas_call x1, Pallas kernels, step(): pl.pallas_call(functools.partial(kernel, (times_n, spaces, fields, depth,...  37.5 us
    add x1, other arithmetic, step(): return ((fine + fix).reshape(starts.shape), slice_norm, total_norm)  2.21 us

commit v1 on v0

--- a/solution.py
+++ b/solution.py
@@ -22,6 +22,7 @@
 PAD = 8
 CHUNK = 16
 LANES = 128
+VMEM_BYTES = 32 * 1024 * 1024
 
 
 def tables(depth, rows, cols, spaces, steps):
@@ -120,11 +121,11 @@
 
 def kernel(
     sizes, starts, source, xf_h, yf_h, zf_h, zi_h, yi_h, xi_h, sym_h,
-    fine_out, fix_out, slice_out, total_out,
-    y1, y2, y3, y4, src, fine, fixes, halo, xf, yf, zf, zi, yi, xi, sym,
+    ends, norms,
+    y1, y2, y3, y4, src, fine, halo, xf, yf, zf, zi, yi, xi, sym,
     own, jumps, ahead, mode_send, mode_recv, square_send, squares,
     load_sem, table_sem, halo_send, halo_recv, ahead_sems, jump_send, jump_recv,
-    mode_ssem, mode_rsem, sq_send, sq_recv, out_sem, relays,
+    mode_ssem, mode_rsem, sq_send, sq_recv, relays,
 ):
     times_n, spaces, fields, depth, rows, cols = sizes
     keep_y, keep_x = rows // 8, cols // 16
@@ -359,8 +360,6 @@
                 if level + 1 < levels:
                     relay(level + 1)
 
-    outs = [pltpu.make_async_copy(fine, fine_out, out_sem.at[0])]
-    outs[0].start()
     spec = transform(lambda l: fine[l])
 
     @pl.when(n < times_n - 1)
@@ -496,11 +495,7 @@
         for p in range(count):
             for i in range(2):
                 l = g * slots + 2 * p + i
-                fixes[l] = fix[p * rows : (p + 1) * rows, i * cols : (i + 1) * cols]
-        held = pl.ds(g * slots, 2 * count)
-        copy = pltpu.make_async_copy(fixes.at[held], fix_out.at[held], out_sem.at[1 + g])
-        copy.start()
-        outs.append(copy)
+                ends[l] = fine[l] + fix[p * rows : (p + 1) * rows, i * cols : (i + 1) * cols]
 
     others(
         lambda k, t, where: square_copy(t * spaces + where, k, (t, where)).wait_recv()
@@ -508,8 +503,8 @@
     cells = fields * depth * spaces * rows * cols
     mine = jnp.sum(squares[pl.ds(n * spaces, spaces)], axis=0)
     every = jnp.sum(squares[...], axis=0)
-    slice_out[0] = jnp.sqrt(mine * (1.0 / cells) + epsilon)[0, 0]
-    total_out[0] = jnp.sqrt(every * (1.0 / (cells * times_n)) + epsilon)[0, 0]
+    norms[0] = jnp.sqrt(mine * (1.0 / cells) + epsilon)
+    norms[1] = jnp.sqrt(every * (1.0 / (cells * times_n)) + epsilon)
 
     others(lambda k, t, where: square_copy(me, k, (t, where)).wait_send())
 
@@ -534,7 +529,16 @@
         lax.fori_loop(0, chunks, drain_halo, 0)
     for offset in range(1, spaces):
         mode_copy(offset).wait_send()
-    for copy in outs:
+
+
+def finish(ends, norms, out, slice_out, total_out, slice_held, total_held, sems):
+    copies = [pltpu.make_async_copy(ends, out, sems.at[0])]
+    copies[0].start()
+    for i, (held, to) in enumerate(((slice_held, slice_out), (total_held, total_out))):
+        held[0] = norms[i, 0, 0]
+        copies.append(pltpu.make_async_copy(held, to, sems.at[1 + i]))
+        copies[-1].start()
+    for copy in copies:
         copy.wait()
 
 
@@ -546,6 +550,7 @@
         keep_y, keep_x = rows // 8, cols // 16
         matrices, symbol = tables(depth, rows, cols, spaces, times_n)
         constants = [halves(t) for t in matrices] + [symbol]
+        operands = [starts, source] + [jnp.asarray(c) for c in constants]
         ky, slot = 2 * keep_y, 2 * keep_x
         groups = -(-fields * depth // (LANES // slot))
         height = groups * ky
@@ -554,25 +559,20 @@
         state = pltpu.VMEM((fields, depth, rows + 2 * PAD, cols), jnp.float32)
         dma = pltpu.SemaphoreType.DMA
         layer_shape = (fields * depth, rows, cols)
-        fine, fix, slice_norm, total_norm = pl.pallas_call(
+        ends, norms = pl.pallas_call(
             functools.partial(kernel, (times_n, spaces, fields, depth, rows, cols)),
             out_shape=(
-                jax.ShapeDtypeStruct(layer_shape, jnp.float32),
-                jax.ShapeDtypeStruct(layer_shape, jnp.float32),
-                jax.ShapeDtypeStruct((1,), jnp.float32),
-                jax.ShapeDtypeStruct((1,), jnp.float32),
+                pltpu.VMEM(layer_shape, jnp.float32),
+                pltpu.VMEM((2, 1, LANES), jnp.float32),
             ),
             in_specs=[pl.BlockSpec(memory_space=pltpu.HBM)] * (2 + len(constants)),
             out_specs=(
-                pl.BlockSpec(memory_space=pl.ANY),
-                pl.BlockSpec(memory_space=pl.ANY),
-                pl.BlockSpec(memory_space=pltpu.SMEM),
-                pl.BlockSpec(memory_space=pltpu.SMEM),
+                pl.BlockSpec(memory_space=pltpu.VMEM),
+                pl.BlockSpec(memory_space=pltpu.VMEM),
             ),
             scratch_shapes=[
                 state, state, state, state,
                 pltpu.VMEM((fields, depth, rows, cols), jnp.float32),
-                pltpu.VMEM(layer_shape, jnp.float32),
                 pltpu.VMEM(layer_shape, jnp.float32),
                 pltpu.VMEM((4, 2, fields, rows, cols), jnp.float32),
                 *[pltpu.VMEM(c.shape, c.dtype) for c in constants],
@@ -587,14 +587,31 @@
                 dma((4, 2, chunks)), dma((4, 2, chunks)), dma((2,)),
                 dma((times_n,)), dma((times_n,)),
                 dma((spaces - 1,)), dma((spaces - 1,)),
-                dma((devices,)), dma((devices,)), dma((2 * fields,)),
+                dma((devices,)), dma((devices,)),
                 pltpu.SemaphoreType.REGULAR(((times_n - 1).bit_length(), 2)),
             ],
             compiler_params=pltpu.CompilerParams(
-                collective_id=0, has_side_effects=True, vmem_limit_bytes=67043328
+                collective_id=0, has_side_effects=True, vmem_limit_bytes=VMEM_BYTES
             ),
-        )(starts, source, *[jnp.asarray(c) for c in constants])
-        return (fine + fix).reshape(starts.shape), slice_norm, total_norm
+        )(*[pltpu.with_memory_space_constraint(a, pltpu.HBM) for a in operands])
+        out, slice_norm, total_norm = pl.pallas_call(
+            finish,
+            out_shape=(
+                jax.ShapeDtypeStruct(layer_shape, jnp.float32),
+                jax.ShapeDtypeStruct((1,), jnp.float32),
+                jax.ShapeDtypeStruct((1,), jnp.float32),
+            ),
+            in_specs=[pl.BlockSpec(memory_space=pltpu.VMEM)] * 2,
+            out_specs=[pl.BlockSpec(memory_space=pltpu.HBM)] * 3,
+            scratch_shapes=[
+                pltpu.SMEM((1,), jnp.float32), pltpu.SMEM((1,), jnp.float32), dma((3,)),
+            ],
+            compiler_params=pltpu.CompilerParams(vmem_limit_bytes=VMEM_BYTES // 2),
+        )(
+            pltpu.with_memory_space_constraint(ends, pltpu.VMEM),
+            pltpu.with_memory_space_constraint(norms, pltpu.VMEM),
+        )
+        return out.reshape(starts.shape), slice_norm, total_norm
 
     return jax.shard_map(
         step,

time: 44.1 us -> 38.5 us (0.87)
  between operations: 4.2 us -> 0.64 us
  other arithmetic: 2.21 us -> 0 us
    add x1 -> x0, other arithmetic: 2.21 us -> none  [step(): return ((fine + fix).reshape(starts.shape), slice_norm, total_norm)]
    pallas_call x0 -> x1, Pallas kernels: none -> 0.88 us  [step(): pl.pallas_call(finish, out_shape=(jax.ShapeDtypeStruct(layer_shape, jnp.f...]
    pallas_call x1, Pallas kernels: 37.5 us -> 36.9 us  [step(): pl.pallas_call(functools.partial(kernel, (times_n, spaces, fields, depth,...]
where the time goes in v1:
time: 38.5 us; the launch traced here: 38.4 us
  Pallas kernels  37.7 us (98%)
  between operations  0.64 us (2%)
    pallas_call x1, Pallas kernels, step(): pl.pallas_call(functools.partial(kernel, (times_n, spaces, fields, depth,...  36.9 us
    pallas_call x1, Pallas kernels, step(): pl.pallas_call(finish, out_shape=(jax.ShapeDtypeStruct(layer_shape, jnp.f...  0.88 us

profile of v1, /device:TPU:0, one launch (start us, length us, event | category | flops | bytes accessed | tf_op | source)
XLA Modules:
  0.0 38.4 jit_solution(13572271543416190854)
XLA Ops:
  0.6 36.9 %shard_map.112 = (f32[20,64,128]{2,1,0:T(8,128)S(1)}, f32[2,1,128]{2,1,0:T(1,128)S(1)}) custom-call(f32[1,5,4,64,128]{4,3,2,1,0:T(8,128)} %starts.1, f32[5,4,64,128]{3,2,1,0:T(8,128)} %source.1, bf16[2,256,128]{2,1,0:T(8,128)(2,1)} %constant.14.clone.xf_h, bf16[2,16,128]{2,1,0:T(8,128)(2,1)} %constant.15.clone.yf_h, ...), custom_call_target="tpu_custom_call" | custom-call | tf_op jit(solution)/shard_map/pallas_call | solution.py:562
  37.5 0.9 %shard_map.113 = (f32[20,64,128]{2,1,0:T(8,128)}, f32[1]{0:T(128)}, f32[1]{0:T(128)}) custom-call(f32[20,64,128]{2,1,0:T(8,128)S(1)} %get-tuple-element.8.ends, f32[2,1,128]{2,1,0:T(1,128)S(1)} %get-tuple-element.9.norms), custom_call_target="tpu_custom_call" | custom-call | tf_op jit(solution)/shard_map/pallas_call | solution.py:597

commit v2 on v1

--- a/solution.py
+++ b/solution.py
@@ -22,13 +22,26 @@
 PAD = 8
 CHUNK = 16
 LANES = 128
+SUBLANES = 8
+PAIR = 2
 VMEM_BYTES = 32 * 1024 * 1024
 
 
-def tables(depth, rows, cols, spaces, steps):
+def layout(fields, depth, rows, cols, times_n, spaces):
+    keep_y, keep_x = rows // 8, cols // 16
+    groups = -(-fields * depth // (LANES // (2 * keep_x)))
+    pair = PAIR if times_n % PAIR == 0 else 1
+    owners = spaces * pair
+    share = 2 * keep_y // owners
+    used = groups * share
+    height = -(-(used + 1) // SUBLANES) * SUBLANES
+    return groups, pair, owners, share, used, height
+
+
+def tables(fields, depth, rows, cols, times_n, spaces):
+    groups, pair, owners, share, used, height = layout(fields, depth, rows, cols, times_n, spaces)
     keep_y, keep_x = rows // 8, cols // 16
     slot = 2 * keep_x
-    per = LANES // (slot * depth)
     full = depth * spaces
     k = np.arange(keep_x)
     x = np.arange(cols)
@@ -46,23 +59,28 @@
     ky = np.where(ky < keep_y, ky, ky - 2 * keep_y)
     y = np.arange(rows)
     ay = 2 * math.pi / rows * ((ky[:, None] * y[None, :]) % rows)
-    yf = np.concatenate([np.cos(ay), np.sin(ay)], axis=1)
-    yi = np.concatenate([np.cos(ay).T, -np.sin(ay).T], axis=1)
     kz = np.arange(full)
     width = full * keep_x
-    half = depth * slot
-    zf = np.zeros((LANES, per * 2 * width))
-    for fp in range(per):
-        for z in range(depth):
-            a = 2 * math.pi / full * ((kz * z) % full)
-            for kk in range(keep_x):
-                row = fp * half + z * slot + kk
-                re = fp * 2 * width + kz * keep_x + kk
-                im = re + width
-                zf[row, re] = np.cos(a)
-                zf[row, im] = -np.sin(a)
-                zf[row + keep_x, re] = np.sin(a)
-                zf[row + keep_x, im] = np.cos(a)
+    block = owners * height
+    yf = np.zeros((block, groups * 2 * rows))
+    yi = np.zeros((groups * rows, 2 * block))
+    for g in range(groups):
+        for at in range(2 * keep_y):
+            row = at // share * height + g * share + at % share
+            yf[row, g * 2 * rows : (g + 1) * 2 * rows] = np.concatenate([np.cos(ay[at]), np.sin(ay[at])])
+            yi[g * rows : (g + 1) * rows, row] = np.cos(ay[at])
+            yi[g * rows : (g + 1) * rows, block + row] = -np.sin(ay[at])
+    zf = np.zeros((full * slot, 2 * width))
+    for z in range(full):
+        a = 2 * math.pi / full * ((kz * z) % full)
+        for kk in range(keep_x):
+            row = z * slot + kk
+            re = kz * keep_x + kk
+            im = re + width
+            zf[row, re] = np.cos(a)
+            zf[row, im] = -np.sin(a)
+            zf[row + keep_x, re] = np.sin(a)
+            zf[row + keep_x, im] = np.cos(a)
     zi = np.zeros((2 * width, full * slot))
     for z in range(full):
         a = 2 * math.pi / full * ((kz * z) % full)
@@ -89,9 +107,12 @@
         + advect_xaxis * np.sin(tx)[None, None, :]
     )
     symbol = (real + 1j * imag) * live
-    powers = np.stack([symbol**p for p in range(1, max(steps, 2))])
-    powers = np.stack([powers.real, powers.imag], axis=1).reshape(-1, 2, 2 * keep_y, width)
-    return [xf, yf, zf, zi, yi, xi], powers.astype(np.float32)
+    symbol = symbol.reshape(owners, share, width)
+    gains = np.zeros((owners, 2, height, width), np.float32)
+    for g in range(groups):
+        gains[:, 0, g * share : (g + 1) * share] = symbol.real
+        gains[:, 1, g * share : (g + 1) * share] = symbol.imag
+    return [xf, yf, zf, zi, yi, xi], gains
 
 
 def halves(table):
@@ -123,22 +144,23 @@
     sizes, starts, source, xf_h, yf_h, zf_h, zi_h, yi_h, xi_h, sym_h,
     ends, norms,
     y1, y2, y3, y4, src, fine, halo, xf, yf, zf, zi, yi, xi, sym,
-    own, jumps, ahead, mode_send, mode_recv, square_send, squares,
+    own, jumps, ahead, gathered, corrections, pieces, modes,
     load_sem, table_sem, halo_send, halo_recv, ahead_sems, jump_send, jump_recv,
-    mode_ssem, mode_rsem, sq_send, sq_recv, relays,
+    mode_send, mode_recv, relays,
 ):
     times_n, spaces, fields, depth, rows, cols = sizes
     keep_y, keep_x = rows // 8, cols // 16
     slot = 2 * keep_x
-    ky = 2 * keep_y
     layers = fields * depth
     slots = LANES // slot
-    groups = -(-layers // slots)
     per = LANES // (slot * depth)
+    groups, pair, owners, share, used, height = layout(fields, depth, rows, cols, times_n, spaces)
     chunks = rows // CHUNK
     n = lax.axis_index("tm")
     s = lax.axis_index("space")
-    me = n * spaces + s
+    place = lax.rem(n, pair)
+    me = place * spaces + s
+    base = n - place
     up = lax.rem(s + 1, spaces)
     down = lax.rem(s + spaces - 1, spaces)
 
@@ -251,9 +273,8 @@
                         piece = pltpu.roll(piece, 2 * p * slot, 1)
                     total = piece if total is None else total + piece
             result.append(total)
-        both = [jnp.concatenate([t, swapped(t)], axis=0) for t in result]
-        spec = under(yf, jnp.concatenate(both, axis=1))
-        return jnp.concatenate([spec[:, g * LANES : (g + 1) * LANES] for g in range(groups)], axis=0)
+        both = jnp.concatenate([part for t in result for part in (t, swapped(t))], axis=0)
+        return under(yf, both).reshape(owners, height, LANES)
 
     for copy in loads[2:] + fills:
         copy.wait()
@@ -362,110 +383,24 @@
 
     spec = transform(lambda l: fine[l])
 
-    @pl.when(n < times_n - 1)
-    def _():
-        ahead_copy.wait_recv()
-        jumps[n] = spec - ahead[...]
-
-    def jump_copy(slot_id, sem_id, target):
+    def jump_copy(index, tile, target):
         return pltpu.make_async_remote_copy(
-            src_ref=jumps.at[slot_id],
-            dst_ref=jumps.at[slot_id],
-            send_sem=jump_send.at[sem_id],
-            recv_sem=jump_recv.at[slot_id],
-            device_id=(target, s),
-            device_id_type=MESH,
-        )
-
-    def send_jump(i, carry):
-        target = times_n - 1 - i
-        jump_copy(n, target, target).start()
-        return carry
-
-    lax.fori_loop(0, times_n - 1 - n, send_jump, 0)
-
-    width = depth * spaces * keep_x
-
-    def collect(i, carry):
-        m = n - 1 - i
-        jump_copy(m, m, n).wait_recv()
-        fresh = times(jumps[m], zf)
-        gain_re = jnp.concatenate([sym[i, 0]] * groups, axis=0)
-        gain_im = jnp.concatenate([sym[i, 1]] * groups, axis=0)
-        result = []
-        for p in range(per):
-            re = fresh[:, 2 * p * width : (2 * p + 1) * width]
-            im = fresh[:, (2 * p + 1) * width : (2 * p + 2) * width]
-            result.append(carry[2 * p] + (gain_re * re - gain_im * im))
-            result.append(carry[2 * p + 1] + (gain_re * im + gain_im * re))
-        return tuple(result)
-
-    zero = jnp.zeros((groups * ky, width), jnp.float32)
-    carry = lax.fori_loop(0, n, collect, (zero,) * (2 * per))
-    stacked = jnp.concatenate(
-        [jnp.concatenate([carry[2 * p], carry[2 * p + 1]], axis=1) for p in range(per)], axis=0
-    )
-    back = times(stacked, zi)
-    half = depth * slot
-    height = groups * ky
-
-    def piece(offset):
-        total = None
-        at = offset * half
-        tile, inside = at // LANES * LANES, at % LANES
-        part = lax.broadcasted_iota(jnp.int32, (1, LANES), 1) // half
-        for p in range(per):
-            block = back[p * height : (p + 1) * height, tile : tile + LANES]
-            move = (p * half - inside) % LANES
-            if move:
-                block = pltpu.roll(block, move, 1)
-            total = block if total is None else jnp.where(part == p, block, total)
-        return total
-
-    def mode_copy(offset):
-        return pltpu.make_async_remote_copy(
-            src_ref=mode_send.at[offset - 1],
-            dst_ref=mode_recv.at[offset - 1],
-            send_sem=mode_ssem.at[offset - 1],
-            recv_sem=mode_rsem.at[offset - 1],
-            device_id=(n, lax.rem(s + offset, spaces)),
-            device_id_type=MESH,
-        )
-
-    for offset in range(1, spaces):
-        mode_send[offset - 1] = piece(offset)
-        mode_copy(offset).start()
-    modes = piece(0)
-    for offset in range(1, spaces):
-        mode_copy(offset).wait_recv()
-        modes = modes + mode_recv[offset - 1]
-
-    weight = jnp.where(lax.rem(lane, keep_x) == 0, 1.0, 2.0)
-    scaled = modes * (1.0 / (depth * spaces * rows * cols))
-    square = jnp.sum(
-        jnp.sum(scaled * scaled * weight, axis=0, keepdims=True), axis=1, keepdims=True
-    ) * float(rows * cols)
-    square_send[...] = jnp.broadcast_to(square, (1, LANES))
-    squares[me] = jnp.broadcast_to(square, (1, LANES))
-
-    def square_copy(index, sem_id, target):
-        return pltpu.make_async_remote_copy(
-            src_ref=square_send,
-            dst_ref=squares.at[index],
-            send_sem=sq_send.at[sem_id],
-            recv_sem=sq_recv.at[index],
+            src_ref=jumps.at[tile],
+            dst_ref=gathered.at[index],
+            send_sem=jump_send.at[target[0] * spaces + target[1]],
+            recv_sem=jump_recv.at[index],
             device_id=target,
             device_id_type=MESH,
         )
 
     def others(act):
         def body(dt, carry):
-            t = n - dt
-            t = jnp.where(t < 0, t + times_n, t)
-            for ds in range(spaces):
+            t = n + dt
+            t = jnp.where(t >= times_n, t - times_n, t)
+            for ds in reversed(range(spaces)):
                 where = s + ds
                 where = jnp.where(where >= spaces, where - spaces, where)
-                run = functools.partial(act, dt * spaces + ds, t, where)
+                run = functools.partial(act, t, where)
                 if ds == 0:
                     pl.when(dt > 0)(run)
                 else:
@@ -473,20 +408,148 @@
             return carry
 
         if times_n <= 8:
-            for dt in range(times_n):
+            for dt in sorted(range(times_n), key=lambda d: -min(d, times_n - d)):
                 body(dt, 0)
         else:
             lax.fori_loop(0, times_n, body, 0)
 
-    others(lambda k, t, where: square_copy(me, k, (t, where)).start())
-
-    both = [
-        jnp.concatenate([t, swapped(t)], axis=0)
-        for t in (modes[g * ky : (g + 1) * ky] for g in range(groups))
+    sent = lambda t, where: jump_copy(
+        n * spaces + s, lax.rem(t, pair) * spaces + where, (t, where)
+    )
+
+    @pl.when(n < times_n - 1)
+    def _():
+        ahead_copy.wait_recv()
+        jumps[...] = spec - ahead[...]
+        others(lambda t, where: sent(t, where).start())
+        gathered[n * spaces + s] = jumps[me]
+
+    def arrive(t, where):
+        @pl.when(t < times_n - 1)
+        def _():
+            jump_copy(t * spaces + where, me, (t, where)).wait_recv()
+
+    others(arrive)
+
+    width = depth * spaces * keep_x
+    half = depth * slot
+    steps = times_n - 1
+    part = lax.broadcasted_iota(jnp.int32, (1, LANES), 1) // half
+
+    def turned(values, move):
+        move = move % LANES
+        return pltpu.roll(values, move, 1) if move else values
+
+    def joined(blocks):
+        total = None
+        for i, block in enumerate(blocks):
+            total = block if total is None else jnp.where(part == i, block, total)
+        return total
+
+    slabs = [
+        jnp.concatenate([gathered[m * spaces + k] for m in range(steps)], axis=0)
+        for k in range(spaces)
     ]
-    planes = under(yi, jnp.concatenate(both, axis=1))
+    lined = [
+        jnp.concatenate(
+            [
+                joined([turned(slabs[at + i], (i - fp) * half) for i in range(per)])
+                for at in range(0, spaces, per)
+            ],
+            axis=1,
+        )
+        for fp in range(per)
+    ]
+    fresh = times(jnp.concatenate(lined, axis=0), zf)
+    gain_re, gain_im = sym[me, 0], sym[me, 1]
+    weight = jnp.where(lax.rem(lane, keep_x) == 0, 1.0, 2.0)
+    zero = jnp.zeros((height, width), jnp.float32)
+    held = [(zero, zero)] * per
+    sizes_of = [jnp.zeros((1, LANES), jnp.float32)]
+    corrections[0] = jnp.zeros((per, height, 2 * width), jnp.float32)
+    for m in range(steps):
+        size = None
+        for fp in range(per):
+            at = (fp * steps + m) * height
+            re = held[fp][0] + fresh[at : at + height, :width]
+            im = held[fp][1] + fresh[at : at + height, width:]
+            re, im = gain_re * re - gain_im * im, gain_re * im + gain_im * re
+            held[fp] = (re, im)
+            corrections[m + 1, fp, :, :width] = re
+            corrections[m + 1, fp, :, width:] = im
+            square = re * re + im * im
+            size = square if size is None else size + square
+        sizes_of.append(jnp.sum(size * weight, axis=0, keepdims=True))
+    back = times(
+        jnp.concatenate([corrections[base + j, fp] for j in range(pair) for fp in range(per)], axis=0), zi
+    )
+    column = jnp.sum(jnp.concatenate(sizes_of, axis=0), axis=1, keepdims=True)
+    shape = (times_n, LANES)
+    diagonal = lax.broadcasted_iota(jnp.int32, shape, 0) == lax.broadcasted_iota(jnp.int32, shape, 1)
+    squares = jnp.sum(jnp.where(diagonal, column, 0.0), axis=0, keepdims=True) * (
+        1.0 / (depth * spaces * rows * cols)
+    )
+    last = lax.broadcasted_iota(jnp.int32, (height, LANES), 0) == used
+    for j in range(pair):
+        for k in range(spaces):
+            at = k * half
+            tile, inside = at // LANES * LANES, at % LANES
+            piece = joined(
+                [
+                    turned(
+                        back[(j * per + fp) * height : (j * per + fp + 1) * height, tile : tile + LANES],
+                        fp * half - inside,
+                    )
+                    for fp in range(per)
+                ]
+            )
+            pieces[j * spaces + k] = jnp.where(last, squares, piece)
+
+    def mode_copy(dj, dk):
+        j, k = lax.rem(place + dj, pair), lax.rem(s + dk, spaces)
+        return pltpu.make_async_remote_copy(
+            src_ref=pieces.at[j * spaces + k],
+            dst_ref=modes.at[me],
+            send_sem=mode_send.at[j * spaces + k],
+            recv_sem=mode_recv.at[me],
+            device_id=(base + j, k),
+            device_id_type=MESH,
+        )
+
+    def mode_arrival(dj, dk):
+        j, k = lax.rem(place + dj, pair), lax.rem(s + dk, spaces)
+        return pltpu.make_async_remote_copy(
+            src_ref=pieces.at[me],
+            dst_ref=modes.at[j * spaces + k],
+            send_sem=mode_send.at[j * spaces + k],
+            recv_sem=mode_recv.at[j * spaces + k],
+            device_id=(base + j, k),
+            device_id_type=MESH,
+        )
+
+    sharers = [(dj, dk) for dj in reversed(range(pair)) for dk in reversed(range(spaces)) if dj + dk]
+    for dj, dk in sharers:
+        mode_copy(dj, dk).start()
+    modes[me] = pieces[me]
+    for dj, dk in sharers:
+        mode_arrival(dj, dk).wait_recv()
+    found = modes[...].reshape(owners * height, LANES)
+    total = None
+    for o in range(owners):
+        row = found[o * height + used : o * height + used + 1]
+        total = row if total is None else total + row
+    cells = fields * depth * spaces * rows * cols
+
+    def norm(values, count):
+        value = jnp.sqrt(jnp.sum(values, axis=1, keepdims=True) * (1.0 / count) + epsilon)
+        return jnp.broadcast_to(value, (1, LANES))
+
+    norms[0] = norm(jnp.where(lane == n, total, 0.0), cells)
+    norms[1] = norm(total, cells * times_n)
+
+    planes = under(yi, jnp.concatenate([found, swapped(found)], axis=0))
     for g in range(groups):
-        plane = planes[:, g * LANES : (g + 1) * LANES]
+        plane = planes[g * rows : (g + 1) * rows]
         count = min(slots, layers - g * slots) // 2
         shifted = [
             plane if p == 0 else pltpu.roll(plane, LANES - 2 * p * slot, 1) for p in range(count)
@@ -497,23 +560,9 @@
                 l = g * slots + 2 * p + i
                 ends[l] = fine[l] + fix[p * rows : (p + 1) * rows, i * cols : (i + 1) * cols]
 
-    others(
-        lambda k, t, where: square_copy(t * spaces + where, k, (t, where)).wait_recv()
-    )
-    cells = fields * depth * spaces * rows * cols
-    mine = jnp.sum(squares[pl.ds(n * spaces, spaces)], axis=0)
-    every = jnp.sum(squares[...], axis=0)
-    norms[0] = jnp.sqrt(mine * (1.0 / cells) + epsilon)
-    norms[1] = jnp.sqrt(every * (1.0 / (cells * times_n)) + epsilon)
-
-    others(lambda k, t, where: square_copy(me, k, (t, where)).wait_send())
-
-    def drain_jump(i, carry):
-        target = times_n - 1 - i
-        jump_copy(n, target, target).wait_send()
-        return carry
-
-    lax.fori_loop(0, times_n - 1 - n, drain_jump, 0)
+    @pl.when(n < times_n - 1)
+    def _():
+        others(lambda t, where: sent(t, where).wait_send())
 
     @pl.when(n > 0)
     def _():
@@ -527,8 +576,8 @@
             return carry
 
         lax.fori_loop(0, chunks, drain_halo, 0)
-    for offset in range(1, spaces):
-        mode_copy(offset).wait_send()
+    for dj, dk in sharers:
+        mode_copy(dj, dk).wait_send()
 
 
 def finish(ends, norms, out, slice_out, total_out, slice_held, total_held, sems):
@@ -547,13 +596,12 @@
 
     def step(starts, source):
         _, fields, depth, rows, cols = starts.shape
-        keep_y, keep_x = rows // 8, cols // 16
-        matrices, symbol = tables(depth, rows, cols, spaces, times_n)
+        matrices, symbol = tables(fields, depth, rows, cols, times_n, spaces)
         constants = [halves(t) for t in matrices] + [symbol]
         operands = [starts, source] + [jnp.asarray(c) for c in constants]
-        ky, slot = 2 * keep_y, 2 * keep_x
-        groups = -(-fields * depth // (LANES // slot))
-        height = groups * ky
+        _, pair, owners, _, _, height = layout(fields, depth, rows, cols, times_n, spaces)
+        slot = cols // 16 * 2
+        per = LANES // (slot * depth)
         chunks = rows // CHUNK
         devices = times_n * spaces
         state = pltpu.VMEM((fields, depth, rows + 2 * PAD, cols), jnp.float32)
@@ -576,18 +624,13 @@
                 pltpu.VMEM(layer_shape, jnp.float32),
                 pltpu.VMEM((4, 2, fields, rows, cols), jnp.float32),
                 *[pltpu.VMEM(c.shape, c.dtype) for c in constants],
-                pltpu.VMEM((height, LANES), jnp.float32),
-                pltpu.VMEM((times_n, height, LANES), jnp.float32),
-                pltpu.VMEM((height, LANES), jnp.float32),
-                pltpu.VMEM((spaces - 1, height, LANES), jnp.float32),
-                pltpu.VMEM((spaces - 1, height, LANES), jnp.float32),
-                pltpu.VMEM((1, LANES), jnp.float32),
-                pltpu.VMEM((devices, 1, LANES), jnp.float32),
+                *[pltpu.VMEM((owners, height, LANES), jnp.float32)] * 3,
+                pltpu.VMEM((devices, height, LANES), jnp.float32),
+                pltpu.VMEM((times_n, per, height, depth * spaces * slot), jnp.float32),
+                *[pltpu.VMEM((owners, height, LANES), jnp.float32)] * 2,
                 dma((6,)), dma((len(constants),)),
                 dma((4, 2, chunks)), dma((4, 2, chunks)), dma((2,)),
-                dma((times_n,)), dma((times_n,)),
-                dma((spaces - 1,)), dma((spaces - 1,)),
-                dma((devices,)), dma((devices,)),
+                dma((devices,)), dma((devices,)), dma((owners,)), dma((owners,)),
                 pltpu.SemaphoreType.REGULAR(((times_n - 1).bit_length(), 2)),
             ],
             compiler_params=pltpu.CompilerParams(

time: 38.5 us -> 34.4 us (0.89)
  Pallas kernels: 37.7 us -> 33.6 us
    pallas_call x1, Pallas kernels: 36.9 us -> 32.7 us  [step(): pl.pallas_call(functools.partial(kernel, (times_n, spaces, fields, depth,...]
where the time goes in v2:
time: 34.4 us; the launch traced here: 34.3 us
  Pallas kernels  33.6 us (98%)
  between operations  0.64 us (2%)
    pallas_call x1, Pallas kernels, step(): pl.pallas_call(functools.partial(kernel, (times_n, spaces, fields, depth,...  32.7 us
    pallas_call x1, Pallas kernels, step(): pl.pallas_call(finish, out_shape=(jax.ShapeDtypeStruct(layer_shape, jnp.f...  0.88 us

profile of v2, /device:TPU:0, one launch (start us, length us, event | category | flops | bytes accessed | tf_op | source)
XLA Modules:
  0.0 34.3 jit_solution(6240476132321014489)
XLA Ops:
  0.6 32.7 %shard_map.112 = (f32[20,64,128]{2,1,0:T(8,128)S(1)}, f32[2,1,128]{2,1,0:T(1,128)S(1)}) custom-call(f32[1,5,4,64,128]{4,3,2,1,0:T(8,128)} %starts.1, f32[5,4,64,128]{3,2,1,0:T(8,128)} %source.1, bf16[2,256,128]{2,1,0:T(8,128)(2,1)} %constant.14.clone.xf_h, bf16[2,64,384]{2,1,0:T(8,128)(2,1)} %constant.15.clone.yf_h, ...), custom_call_target="tpu_custom_call" | custom-call | tf_op jit(solution)/shard_map/pallas_call | solution.py:610
  33.4 0.9 %shard_map.113 = (f32[20,64,128]{2,1,0:T(8,128)}, f32[1]{0:T(128)}, f32[1]{0:T(128)}) custom-call(f32[20,64,128]{2,1,0:T(8,128)S(1)} %get-tuple-element.8.ends, f32[2,1,128]{2,1,0:T(1,128)S(1)} %get-tuple-element.9.norms), custom_call_target="tpu_custom_call" | custom-call | tf_op jit(solution)/shard_map/pallas_call | solution.py:640

commit v3 on v2

--- a/solution.py
+++ b/solution.py
@@ -231,8 +231,8 @@
         return pltpu.make_async_remote_copy(
             src_ref=state.at[:, layer, pl.ds(pl.multiple_of(PAD + r0, 8), CHUNK)],
             dst_ref=halo.at[stage, side, :, pl.ds(r0, CHUNK)],
-            send_sem=halo_send.at[stage, side, chunk],
-            recv_sem=halo_recv.at[stage, side, chunk],
+            send_sem=halo_send,
+            recv_sem=halo_recv.at[stage % 2, side, chunk],
             device_id=(n, up if side == 0 else down),
             device_id_type=MESH,
         )
@@ -387,8 +387,8 @@
         return pltpu.make_async_remote_copy(
             src_ref=jumps.at[tile],
             dst_ref=gathered.at[index],
-            send_sem=jump_send.at[target[0] * spaces + target[1]],
-            recv_sem=jump_recv.at[index],
+            send_sem=jump_send,
+            recv_sem=jump_recv,
             device_id=target,
             device_id_type=MESH,
         )
@@ -424,12 +424,14 @@
         others(lambda t, where: sent(t, where).start())
         gathered[n * spaces + s] = jumps[me]
 
-    def arrive(t, where):
-        @pl.when(t < times_n - 1)
-        def _():
-            jump_copy(t * spaces + where, me, (t, where)).wait_recv()
-
-    others(arrive)
+    def settle(ref, count, sem):
+        held = ref if count is None else ref.at[pl.ds(0, count)]
+        pltpu.make_async_copy(held, held, sem).wait()
+
+    pl.when(n < times_n - 1)(
+        lambda: settle(gathered, (times_n - 1) * spaces - 1, jump_recv)
+    )
+    pl.when(n == times_n - 1)(lambda: settle(gathered, (times_n - 1) * spaces, jump_recv))
 
     width = depth * spaces * keep_x
     half = depth * slot
@@ -510,19 +512,8 @@
         return pltpu.make_async_remote_copy(
             src_ref=pieces.at[j * spaces + k],
             dst_ref=modes.at[me],
-            send_sem=mode_send.at[j * spaces + k],
-            recv_sem=mode_recv.at[me],
-            device_id=(base + j, k),
-            device_id_type=MESH,
-        )
-
-    def mode_arrival(dj, dk):
-        j, k = lax.rem(place + dj, pair), lax.rem(s + dk, spaces)
-        return pltpu.make_async_remote_copy(
-            src_ref=pieces.at[me],
-            dst_ref=modes.at[j * spaces + k],
-            send_sem=mode_send.at[j * spaces + k],
-            recv_sem=mode_recv.at[j * spaces + k],
+            send_sem=mode_send,
+            recv_sem=mode_recv,
             device_id=(base + j, k),
             device_id_type=MESH,
         )
@@ -531,8 +522,7 @@
     for dj, dk in sharers:
         mode_copy(dj, dk).start()
     modes[me] = pieces[me]
-    for dj, dk in sharers:
-        mode_arrival(dj, dk).wait_recv()
+    settle(modes, owners - 1, mode_recv)
     found = modes[...].reshape(owners * height, LANES)
     total = None
     for o in range(owners):
@@ -560,24 +550,14 @@
                 l = g * slots + 2 * p + i
                 ends[l] = fine[l] + fix[p * rows : (p + 1) * rows, i * cols : (i + 1) * cols]
 
-    @pl.when(n < times_n - 1)
-    def _():
-        others(lambda t, where: sent(t, where).wait_send())
+    pl.when(n < times_n - 1)(lambda: settle(gathered, times_n * spaces - 1, jump_send))
 
     @pl.when(n > 0)
     def _():
         ahead_copy.wait_send()
 
-    for stage in range(4):
-
-        def drain_halo(c, carry):
-            for side in range(2):
-                halo_copy(stage, side, c).wait_send()
-            return carry
-
-        lax.fori_loop(0, chunks, drain_halo, 0)
-    for dj, dk in sharers:
-        mode_copy(dj, dk).wait_send()
+    settle(halo, None, halo_send)
+    settle(modes, owners - 1, mode_send)
 
 
 def finish(ends, norms, out, slice_out, total_out, slice_held, total_held, sems):
@@ -629,8 +609,7 @@
                 pltpu.VMEM((times_n, per, height, depth * spaces * slot), jnp.float32),
                 *[pltpu.VMEM((owners, height, LANES), jnp.float32)] * 2,
                 dma((6,)), dma((len(constants),)),
-                dma((4, 2, chunks)), dma((4, 2, chunks)), dma((2,)),
-                dma((devices,)), dma((devices,)), dma((owners,)), dma((owners,)),
+                dma, dma((2, 2, chunks)), dma((2,)), dma, dma, dma, dma,
                 pltpu.SemaphoreType.REGULAR(((times_n - 1).bit_length(), 2)),
             ],
             compiler_params=pltpu.CompilerParams(

time: 34.4 us -> 33 us (0.959)
  Pallas kernels: 33.6 us -> 32.2 us
    pallas_call x1, Pallas kernels: 32.7 us -> 31.4 us  [step(): pl.pallas_call(functools.partial(kernel, (times_n, spaces, fields, depth,...]
where the time goes in v3:
time: 33 us; the launch traced here: 32.9 us
  Pallas kernels  32.2 us (98%)
  between operations  0.64 us (2%)
    pallas_call x1, Pallas kernels, step(): pl.pallas_call(functools.partial(kernel, (times_n, spaces, fields, depth,...  31.4 us
    pallas_call x1, Pallas kernels, step(): pl.pallas_call(finish, out_shape=(jax.ShapeDtypeStruct(layer_shape, jnp.f...  0.88 us

profile of v3, /device:TPU:0, one launch (start us, length us, event | category | flops | bytes accessed | tf_op | source)
XLA Modules:
  0.0 32.9 jit_solution(9790521955913096956)
XLA Ops:
  0.6 31.4 %shard_map.112 = (f32[20,64,128]{2,1,0:T(8,128)S(1)}, f32[2,1,128]{2,1,0:T(1,128)S(1)}) custom-call(f32[1,5,4,64,128]{4,3,2,1,0:T(8,128)} %starts.1, f32[5,4,64,128]{3,2,1,0:T(8,128)} %source.1, bf16[2,256,128]{2,1,0:T(8,128)(2,1)} %constant.14.clone.xf_h, bf16[2,64,384]{2,1,0:T(8,128)(2,1)} %constant.15.clone.yf_h, ...), custom_call_target="tpu_custom_call" | custom-call | tf_op jit(solution)/shard_map/pallas_call | solution.py:590
  32.0 0.9 %shard_map.113 = (f32[20,64,128]{2,1,0:T(8,128)}, f32[1]{0:T(128)}, f32[1]{0:T(128)}) custom-call(f32[20,64,128]{2,1,0:T(8,128)S(1)} %get-tuple-element.8.ends, f32[2,1,128]{2,1,0:T(1,128)S(1)} %get-tuple-element.9.norms), custom_call_target="tpu_custom_call" | custom-call | tf_op jit(solution)/shard_map/pallas_call | solution.py:619

commit v4 on v3

--- a/solution.py
+++ b/solution.py
@@ -34,7 +34,7 @@
     owners = spaces * pair
     share = 2 * keep_y // owners
     used = groups * share
-    height = -(-(used + 1) // SUBLANES) * SUBLANES
+    height = -(-max(used + 1, used + share) // SUBLANES) * SUBLANES
     return groups, pair, owners, share, used, height
 
 
@@ -62,12 +62,15 @@
     kz = np.arange(full)
     width = full * keep_x
     block = owners * height
-    yf = np.zeros((block, groups * 2 * rows))
+    yf = np.zeros((block, (groups + 1) * 2 * rows))
     yi = np.zeros((groups * rows, 2 * block))
+    for g in range(groups + 1):
+        for at in range(2 * keep_y):
+            row = at // share * height + g * share + at % share
+            yf[row, g * 2 * rows : (g + 1) * 2 * rows] = np.concatenate([np.cos(ay[at]), np.sin(ay[at])])
     for g in range(groups):
         for at in range(2 * keep_y):
             row = at // share * height + g * share + at % share
-            yf[row, g * 2 * rows : (g + 1) * 2 * rows] = np.concatenate([np.cos(ay[at]), np.sin(ay[at])])
             yi[g * rows : (g + 1) * rows, row] = np.cos(ay[at])
             yi[g * rows : (g + 1) * rows, block + row] = -np.sin(ay[at])
     zf = np.zeros((full * slot, 2 * width))
@@ -108,10 +111,12 @@
     )
     symbol = (real + 1j * imag) * live
     symbol = symbol.reshape(owners, share, width)
-    gains = np.zeros((owners, 2, height, width), np.float32)
-    for g in range(groups):
-        gains[:, 0, g * share : (g + 1) * share] = symbol.real
-        gains[:, 1, g * share : (g + 1) * share] = symbol.imag
+    per = LANES // (slot * depth)
+    gains = np.zeros((owners, per, 2, height, width), np.float32)
+    for f in range(fields):
+        at = f // per * share
+        gains[:, f % per, 0, at : at + share] = symbol.real
+        gains[:, f % per, 1, at : at + share] = symbol.imag
     return [xf, yf, zf, zi, yi, xi], gains
 
 
@@ -143,7 +148,7 @@
 def kernel(
     sizes, starts, source, xf_h, yf_h, zf_h, zi_h, yi_h, xi_h, sym_h,
     ends, norms,
-    y1, y2, y3, y4, src, fine, halo, xf, yf, zf, zi, yi, xi, sym,
+    y1, y2, y3, y4, src, fine, rims, halo, xf, yf, zf, zi, yi, xi, sym,
     own, jumps, ahead, gathered, corrections, pieces, modes,
     load_sem, table_sem, halo_send, halo_recv, ahead_sems, jump_send, jump_recv,
     mode_send, mode_recv, relays,
@@ -253,33 +258,37 @@
             first, pltpu.roll(values, LANES - keep_x, 1), -pltpu.roll(values, keep_x, 1)
         )
 
-    def transform(layer_of):
-        pairs = jnp.concatenate(
-            [
-                jnp.concatenate([layer_of(2 * p), layer_of(2 * p + 1)], axis=1)
-                for p in range(layers // 2)
-            ],
-            axis=0,
-        )
-        packed = times(pairs, xf)
-        result = []
-        for g in range(groups):
-            total = None
-            for p in range(slots // 2):
-                index = g * (slots // 2) + p
-                if index < layers // 2:
-                    piece = packed[index * rows : (index + 1) * rows]
-                    if p > 0:
-                        piece = pltpu.roll(piece, 2 * p * slot, 1)
-                    total = piece if total is None else total + piece
-            result.append(total)
+    def transform(pairs, count):
+        stacked = jnp.concatenate(
+            [jnp.concatenate([left, right], axis=1) for _, _, left, right in pairs], axis=0
+        )
+        packed = times(stacked, xf)
+        result = [None] * count
+        for i, (g, at, _, _) in enumerate(pairs):
+            piece = packed[i * rows : (i + 1) * rows]
+            if at > 0:
+                piece = pltpu.roll(piece, at * slot, 1)
+            result[g] = piece if result[g] is None else result[g] + piece
         both = jnp.concatenate([part for t in result for part in (t, swapped(t))], axis=0)
-        return under(yf, both).reshape(owners, height, LANES)
+        table = [yf[i, :, : count * 2 * rows] for i in range(2)]
+        return under(table, both).reshape(owners, height, LANES)
+
+    def paired(layer_of):
+        return [
+            (l // slots, l % slots, layer_of(l), layer_of(l + 1)) for l in range(0, layers, 2)
+        ]
+
+    def rim_place(f):
+        if f // per == groups - 1 and fields % per:
+            return groups - 1, fields % per * depth
+        return groups, f % per * depth + 2 * (f // per)
 
     for copy in loads[2:] + fills:
         copy.wait()
 
-    own[...] = transform(lambda l: y1[l // depth, l % depth, pl.ds(PAD, rows)])
+    own[...] = transform(
+        paired(lambda l: y1[l // depth, l % depth, pl.ds(PAD, rows)]), groups
+    )
     ahead_copy = pltpu.make_async_remote_copy(
         src_ref=own,
         dst_ref=ahead,
@@ -293,7 +302,18 @@
     def _():
         ahead_copy.start()
 
-    def update(stage, z, r0, below, above):
+    shift = viscosity - diffusivity
+
+    def reach(layer, sign):
+        factor = (viscosity + sign * 0.5 * advect_zaxis) + (sign * 0.5) * layer[2]
+        result = [factor * layer[f] for f in range(3)]
+        result[2] = result[2] + (sign * 0.5) * layer[3]
+        return result + [(sign * 0.5 * compress_rate) * layer[2], (factor - shift) * layer[4]]
+
+    def weigh(stage):
+        return time_step / 6.0 * (1.0, 2.0, 2.0, 1.0)[stage]
+
+    def update(stage, z, r0, below, above, rim=None):
         state = states[stage]
         mid, xm, xp, ym, yp = [], [], [], [], []
         rolled = CHUNK + 2 * PAD
@@ -305,36 +325,49 @@
             yp.append(pltpu.roll(wide, rolled - 1, 0)[PAD : PAD + CHUNK])
             xm.append(pltpu.roll(centre, 1, 1))
             xp.append(pltpu.roll(centre, cols - 1, 1))
-        zm = [below(f) for f in range(fields)]
-        zp = [above(f) for f in range(fields)]
-        sides = [xm, xp, ym, yp, zm, zp]
-        factors = []
-        for axis, speed in enumerate((advect_xaxis, advect_yaxis, advect_zaxis)):
-            factors.append((viscosity + 0.5 * speed) + 0.5 * sides[2 * axis][axis])
-            factors.append((viscosity - 0.5 * speed) - 0.5 * sides[2 * axis + 1][axis])
-        shift = viscosity - diffusivity
+        sides = [(xm, 0, 1.0, advect_xaxis), (xp, 0, -1.0, advect_xaxis)]
+        sides += [(ym, 1, 1.0, advect_yaxis), (yp, 1, -1.0, advect_yaxis)]
+        for neighbour, sign in ((below, 1.0), (above, -1.0)):
+            if neighbour is not None:
+                held = [neighbour(f) for f in range(fields)]
+                sides.append((held, 2, sign, advect_zaxis))
+        factors = [
+            (viscosity + sign * 0.5 * speed) + (sign * 0.5) * side[axis]
+            for side, axis, sign, speed in sides
+        ]
         rates = []
         for f in range(fields):
             forcing = src[f, z, pl.ds(r0, CHUNK)]
             if f == 3:
-                total = (
-                    (xp[0] - xm[0]) + (yp[1] - ym[1]) + (zp[2] - zm[2])
-                ) * (-0.5 * compress_rate)
+                total = None
+                for side, axis, sign, _ in sides:
+                    if total is None:
+                        total = side[axis]
+                    else:
+                        total = total + side[axis] if sign > 0 else total - side[axis]
+                total = total * (0.5 * compress_rate)
             else:
                 gain = viscosity if f < 3 else diffusivity
                 total = (-6.0 * gain) * mid[f]
-                for factor, side in zip(factors, sides):
+                push = None
+                for factor, (side, axis, sign, _) in zip(factors, sides):
                     total = total + (factor if f < 3 else factor - shift) * side[f]
-                if f < 3:
-                    total = total + 0.5 * (sides[2 * f][3] - sides[2 * f + 1][3])
+                    if axis == f:
+                        term = (sign * 0.5) * side[3]
+                        push = term if push is None else push + term
+                if push is not None:
+                    total = total + push
             rates.append(total + forcing)
-        share = time_step / 6.0 * (1.0, 2.0, 2.0, 1.0)[stage]
+        share_of = weigh(stage)
+        if rim is not None:
+            for f, value in enumerate(reach(mid, 1.0 if rim else -1.0)):
+                rims[rim, f, pl.ds(r0, CHUNK)] = share_of * value
         for f in range(fields):
             at = f * depth + z
             here = pl.ds(r0, CHUNK)
             begin = y1[f, z, pl.ds(pl.multiple_of(r0 + PAD, 8), CHUNK)]
             done = begin if stage == 0 else fine[at, here]
-            fine[at, here] = done + share * rates[f]
+            fine[at, here] = done + share_of * rates[f]
             if stage < 3:
                 later = states[stage + 1]
                 step = (0.5, 0.5, 1.0)[stage] * time_step
@@ -363,13 +396,19 @@
             r0 = pl.multiple_of(c * CHUNK, CHUNK)
             at = pl.ds(pl.multiple_of(r0 + PAD, 8), CHUNK)
             for side in range(2):
+                if stage == 3:
+                    if side == 0:
+                        update(stage, 0, r0, None, lambda f: state[f, 1, at], side)
+                    else:
+                        update(stage, depth - 1, r0, lambda f: state[f, depth - 2, at], None, side)
+                    continue
                 halo_copy(stage, side, c).wait_recv()
                 here = lambda f: halo[stage, side, f, pl.ds(r0, CHUNK)]
                 if side == 0:
                     update(stage, 0, r0, here, lambda f: state[f, 1, at])
                 else:
                     update(stage, depth - 1, r0, lambda f: state[f, depth - 2, at], here)
-                if stage < 3:
+                if stage < 2:
                     halo_copy(stage + 1, 1 - side, c).start()
             return carry
 
@@ -381,7 +420,10 @@
                 if level + 1 < levels:
                     relay(level + 1)
 
-    spec = transform(lambda l: fine[l])
+    spec = transform(
+        paired(lambda l: fine[l]) + [(*rim_place(f), rims[1, f], rims[0, f]) for f in range(fields)],
+        groups + 1,
+    )
 
     def jump_copy(index, tile, target):
         return pltpu.make_async_remote_copy(
@@ -424,6 +466,23 @@
         others(lambda t, where: sent(t, where).start())
         gathered[n * spaces + s] = jumps[me]
 
+    def send_last(c, carry):
+        for side in range(2):
+            halo_copy(3, side, c).start()
+        return carry
+
+    def finish_edge(c, carry):
+        here = pl.ds(pl.multiple_of(c * CHUNK, CHUNK), CHUNK)
+        for side in range(2):
+            halo_copy(3, side, c).wait_recv()
+            layer = [halo[3, side, f, here] for f in range(fields)]
+            for f, value in enumerate(reach(layer, -1.0 if side else 1.0)):
+                at = f * depth + side * (depth - 1)
+                fine[at, here] = fine[at, here] + weigh(3) * value
+        return carry
+
+    lax.fori_loop(0, chunks, send_last, 0)
+
     def settle(ref, count, sem):
         held = ref if count is None else ref.at[pl.ds(0, count)]
         pltpu.make_async_copy(held, held, sem).wait()
@@ -448,10 +507,31 @@
             total = block if total is None else jnp.where(part == i, block, total)
         return total
 
-    slabs = [
-        jnp.concatenate([gathered[m * spaces + k] for m in range(steps)], axis=0)
-        for k in range(spaces)
+    place_of = lax.rem(lax.broadcasted_iota(jnp.int32, (1, 1, LANES), 2), half) // slot
+    line_of = lax.broadcasted_iota(jnp.int32, (1, height, 1), 1) // share
+    raw = [
+        jnp.stack([gathered[m * spaces + k] for m in range(steps)], axis=0) for k in range(spaces)
     ]
+
+    def slid(values, move, axis):
+        move = move % values.shape[axis]
+        return pltpu.roll(values, move, axis) if move else values
+
+    def rim_values(values):
+        total = None
+        for f in range(0, fields, per):
+            g, at = rim_place(f)
+            moved = slid(slid(values, -(at - f % per * depth) * slot, 2), (f // per - g) * share, 1)
+            total = moved if total is None else jnp.where(line_of == f // per, moved, total)
+        return total
+
+    reached = [rim_values(values) for values in raw]
+    slabs = []
+    for k in range(spaces):
+        from_below = jnp.where(place_of == 0, reached[(k - 1) % spaces], 0.0)
+        from_above = slid(reached[(k + 1) % spaces], (depth - 2) * slot, 2)
+        from_above = jnp.where(place_of == depth - 1, from_above, 0.0)
+        slabs.append((raw[k] + (from_below + from_above)).reshape(steps * height, LANES))
     lined = [
         jnp.concatenate(
             [
@@ -463,7 +543,7 @@
         for fp in range(per)
     ]
     fresh = times(jnp.concatenate(lined, axis=0), zf)
-    gain_re, gain_im = sym[me, 0], sym[me, 1]
+    gains = [(sym[me, fp, 0], sym[me, fp, 1]) for fp in range(per)]
     weight = jnp.where(lax.rem(lane, keep_x) == 0, 1.0, 2.0)
     zero = jnp.zeros((height, width), jnp.float32)
     held = [(zero, zero)] * per
@@ -475,6 +555,7 @@
             at = (fp * steps + m) * height
             re = held[fp][0] + fresh[at : at + height, :width]
             im = held[fp][1] + fresh[at : at + height, width:]
+            gain_re, gain_im = gains[fp]
             re, im = gain_re * re - gain_im * im, gain_re * im + gain_im * re
             held[fp] = (re, im)
             corrections[m + 1, fp, :, :width] = re
@@ -522,6 +603,7 @@
     for dj, dk in sharers:
         mode_copy(dj, dk).start()
     modes[me] = pieces[me]
+    lax.fori_loop(0, chunks, finish_edge, 0)
     settle(modes, owners - 1, mode_recv)
     found = modes[...].reshape(owners * height, LANES)
     total = None
@@ -602,6 +684,7 @@
                 state, state, state, state,
                 pltpu.VMEM((fields, depth, rows, cols), jnp.float32),
                 pltpu.VMEM(layer_shape, jnp.float32),
+                pltpu.VMEM((2, fields, rows, cols), jnp.float32),
                 pltpu.VMEM((4, 2, fields, rows, cols), jnp.float32),
                 *[pltpu.VMEM(c.shape, c.dtype) for c in constants],
                 *[pltpu.VMEM((owners, height, LANES), jnp.float32)] * 3,

time: 33 us -> 31 us (0.939)
  Pallas kernels: 32.2 us -> 30.2 us
    pallas_call x1, Pallas kernels: 31.4 us -> 29.4 us  [step(): pl.pallas_call(functools.partial(kernel, (times_n, spaces, fields, depth,...]
where the time goes in v4:
time: 31 us; the launch traced here: 30.9 us
  Pallas kernels  30.2 us (97%)
  between operations  0.64 us (2%)
    pallas_call x1, Pallas kernels, step(): pl.pallas_call(functools.partial(kernel, (times_n, spaces, fields, depth,...  29.4 us
    pallas_call x1, Pallas kernels, step(): pl.pallas_call(finish, out_shape=(jax.ShapeDtypeStruct(layer_shape, jnp.f...  0.88 us

profile of v4, /device:TPU:0, one launch (start us, length us, event | category | flops | bytes accessed | tf_op | source)
XLA Modules:
  0.0 30.9 jit_solution(12925026606872995394)
XLA Ops:
  0.6 29.4 %shard_map.112 = (f32[20,64,128]{2,1,0:T(8,128)S(1)}, f32[2,1,128]{2,1,0:T(1,128)S(1)}) custom-call(f32[1,5,4,64,128]{4,3,2,1,0:T(8,128)} %starts.1, f32[5,4,64,128]{3,2,1,0:T(8,128)} %source.1, bf16[2,256,128]{2,1,0:T(8,128)(2,1)} %constant.14.clone.xf_h, bf16[2,64,512]{2,1,0:T(8,128)(2,1)} %constant.15.clone.yf_h, ...), custom_call_target="tpu_custom_call" | custom-call | tf_op jit(solution)/shard_map/pallas_call | solution.py:672
  30.0 0.9 %shard_map.113 = (f32[20,64,128]{2,1,0:T(8,128)}, f32[1]{0:T(128)}, f32[1]{0:T(128)}) custom-call(f32[20,64,128]{2,1,0:T(8,128)S(1)} %get-tuple-element.8.ends, f32[2,1,128]{2,1,0:T(1,128)S(1)} %get-tuple-element.9.norms), custom_call_target="tpu_custom_call" | custom-call | tf_op jit(solution)/shard_map/pallas_call | solution.py:702

commit v5 on v4

--- a/solution.py
+++ b/solution.py
@@ -117,13 +117,23 @@
         at = f // per * share
         gains[:, f % per, 0, at : at + share] = symbol.real
         gains[:, f % per, 1, at : at + share] = symbol.imag
-    return [xf, yf, zf, zi, yi, xi], gains
-
-
-def halves(table):
+    held = {
+        "xf": halves(xf, 1), "yf": halves(yf, 1), "zf": halves(zf, 1), "zi": halves(zi, 1),
+        "yi": halves(yi, 1, True), "xi": halves(xi, 0, True),
+    }
+    places, at, blocks = {}, 0, []
+    for name, table in held.items():
+        height, wide = table.shape
+        places[name] = (at, height, wide // LANES)
+        blocks += [table[:, i : i + LANES] for i in range(0, wide, LANES)]
+        at += height * (wide // LANES)
+    return places, np.concatenate(blocks, axis=0), gains
+
+
+def halves(table, axis, twice=False):
     high = table.astype(jnp.bfloat16)
     low = (table - high.astype(np.float64)).astype(jnp.bfloat16)
-    return np.stack([high, low])
+    return np.concatenate([high, high, low] if twice else [high, low], axis=axis)
 
 
 def split(values):
@@ -137,18 +147,36 @@
 
 def times(values, table):
     high, low = split(values)
-    return dot(high, table[0]) + dot(low, table[0]) + dot(high, table[1])
+    wide = table.shape[1] // 2
+    if wide > LANES:
+        return dot(high, table[:, :wide]) + dot(low, table[:, :wide]) + dot(high, table[:, wide:])
+    both = dot(high, table)
+    return both[:, :wide] + dot(low, table[:, :wide]) + both[:, wide:]
+
+
+def times_deep(values, table):
+    high, low = split(values)
+    deep = 2 * values.shape[1]
+    return dot(jnp.concatenate([high, low], axis=1), table[:deep]) + dot(high, table[deep:])
 
 
 def under(table, values):
     high, low = split(values)
-    return dot(table[0], high) + dot(table[0], low) + dot(table[1], high)
+    deep, wide = values.shape
+    both = dot(table[:, :deep], jnp.concatenate([high, low], axis=1))
+    return both[:, :wide] + both[:, wide:] + dot(table[:, deep:], high)
+
+
+def under_deep(table, values):
+    high, low = split(values)
+    deep = 2 * values.shape[0]
+    return dot(table[:, :deep], jnp.concatenate([high, low], axis=0)) + dot(table[:, deep:], high)
 
 
 def kernel(
-    sizes, starts, source, xf_h, yf_h, zf_h, zi_h, yi_h, xi_h, sym_h,
+    sizes, places, starts, source, tables_h, sym_h,
     ends, norms,
-    y1, y2, y3, y4, src, fine, rims, halo, xf, yf, zf, zi, yi, xi, sym,
+    y1, y2, y3, y4, src, fine, rims, late, begun, table, sym,
     own, jumps, ahead, gathered, corrections, pieces, modes,
     load_sem, table_sem, halo_send, halo_recv, ahead_sems, jump_send, jump_recv,
     mode_send, mode_recv, relays,
@@ -181,35 +209,25 @@
     for offset in range(1, spaces):
         enter(n, lax.rem(s + offset, spaces))
     near(1, lambda side, target: enter(target, s))
+    edges = [
+        pltpu.make_async_copy(
+            starts.at[0, :, z], y1.at[:, z + 1, pl.ds(PAD, rows)], load_sem.at[min(z, 1)]
+        )
+        for z in (0, depth - 1)
+    ]
+    for copy in edges:
+        copy.start()
     loads = [
-        pltpu.make_async_copy(starts.at[0, :, 0], y1.at[:, 0, pl.ds(PAD, rows)], load_sem.at[0]),
-        pltpu.make_async_copy(
-            starts.at[0, :, depth - 1], y1.at[:, depth - 1, pl.ds(PAD, rows)], load_sem.at[4]
-        ),
         pltpu.make_async_copy(
             starts.at[0, :, pl.ds(1, depth - 2)],
-            y1.at[:, pl.ds(1, depth - 2), pl.ds(PAD, rows)],
-            load_sem.at[5],
+            y1.at[:, pl.ds(2, depth - 2), pl.ds(PAD, rows)],
+            load_sem.at[2],
         ),
-        pltpu.make_async_copy(
-            starts.at[0, :, :, pl.ds(rows - PAD, PAD)], y1.at[:, :, pl.ds(0, PAD)], load_sem.at[1]
-        ),
-        pltpu.make_async_copy(
-            starts.at[0, :, :, pl.ds(0, PAD)], y1.at[:, :, pl.ds(PAD + rows, PAD)], load_sem.at[2]
-        ),
+        pltpu.make_async_copy(tables_h, table, table_sem.at[0]),
         pltpu.make_async_copy(source, src, load_sem.at[3]),
+        pltpu.make_async_copy(sym_h, sym, table_sem.at[1]),
     ]
-    for copy in loads:
-        copy.start()
-    fills = [
-        pltpu.make_async_copy(a, b, table_sem.at[i])
-        for i, (a, b) in enumerate(
-            [(xf_h, xf), (yf_h, yf), (zf_h, zf), (zi_h, zi), (yi_h, yi), (xi_h, xi), (sym_h, sym)]
-        )
-    ]
-    for copy in fills:
-        copy.start()
-    for copy in loads[:2]:
+    for copy in edges:
         copy.wait()
     beside = jnp.where(n > 0, 1, 0) + jnp.where(n < times_n - 1, 1, 0)
     pl.semaphore_wait(barrier, spaces - 1 + beside)
@@ -229,25 +247,47 @@
 
     states = [y1, y2, y3, y4]
 
-    def halo_copy(stage, side, chunk):
-        r0 = pl.multiple_of(chunk * CHUNK, CHUNK)
-        state = states[stage]
-        layer = depth - 1 if side == 0 else 0
-        return pltpu.make_async_remote_copy(
-            src_ref=state.at[:, layer, pl.ds(pl.multiple_of(PAD + r0, 8), CHUNK)],
-            dst_ref=halo.at[stage, side, :, pl.ds(r0, CHUNK)],
-            send_sem=halo_send,
-            recv_sem=halo_recv.at[stage % 2, side, chunk],
-            device_id=(n, up if side == 0 else down),
+    parity = lax.rem(s, 2)
+    far_to, near_to = jnp.where(parity == 0, down, up), jnp.where(parity == 0, up, down)
+    far_z = jnp.where(parity == 0, 1, depth)
+    near_z = depth + 1 - far_z
+    step = 1 - 2 * parity
+    far_halo, near_halo = far_z - step, near_z + step
+
+    def settle(held, sem):
+        pltpu.make_async_copy(held, held, sem).wait()
+
+    def span(chunk):
+        return pl.ds(pl.multiple_of(PAD + chunk * CHUNK, PAD), CHUNK)
+
+    def send(src_ref, dst_ref, stage, index, target):
+        pltpu.make_async_remote_copy(
+            src_ref=src_ref,
+            dst_ref=dst_ref,
+            send_sem=halo_send.at[stage],
+            recv_sem=halo_recv.at[stage % 2, index],
+            device_id=(n, target),
             device_id_type=MESH,
+        ).start()
+
+    def send_near(stage):
+        here, state = pl.ds(PAD, rows), states[stage]
+        send(state.at[:, near_z, here], state.at[:, depth + 1 - near_halo, here], stage, 0, near_to)
+
+    def send_far(stage, chunk):
+        here, state = span(chunk), states[stage]
+        send(
+            state.at[:, far_z, here], state.at[:, depth + 1 - far_halo, here], stage, 1 + chunk, far_to
         )
 
     def send_first(c, carry):
-        for side in range(2):
-            halo_copy(0, side, c).start()
+        send_far(0, c)
         return carry
 
     lax.fori_loop(0, chunks, send_first, 0)
+    send_near(0)
+    for copy in loads:
+        copy.start()
     relay(0)
 
     lane = lax.broadcasted_iota(jnp.int32, (1, LANES), 1)
@@ -258,24 +298,39 @@
             first, pltpu.roll(values, LANES - keep_x, 1), -pltpu.roll(values, keep_x, 1)
         )
 
-    def transform(pairs, count):
+    def entry(name):
+        at, height_of, wide = places[name]
+        return jnp.concatenate(
+            [table[pl.ds(at + i * height_of, height_of)] for i in range(wide)], axis=1
+        )
+
+    def pack(pairs, result):
         stacked = jnp.concatenate(
             [jnp.concatenate([left, right], axis=1) for _, _, left, right in pairs], axis=0
         )
-        packed = times(stacked, xf)
-        result = [None] * count
+        packed = times(stacked, entry("xf"))
+        result = list(result)
         for i, (g, at, _, _) in enumerate(pairs):
             piece = packed[i * rows : (i + 1) * rows]
-            if at > 0:
+            if not (isinstance(at, int) and at == 0):
                 piece = pltpu.roll(piece, at * slot, 1)
             result[g] = piece if result[g] is None else result[g] + piece
+        return result
+
+    def transform(result):
         both = jnp.concatenate([part for t in result for part in (t, swapped(t))], axis=0)
-        table = [yf[i, :, : count * 2 * rows] for i in range(2)]
-        return under(table, both).reshape(owners, height, LANES)
-
-    def paired(layer_of):
+        at, tall, wide = places["yf"]
+        blocks = wide // 2
+        held = len(result) * 2 * rows // LANES
+        columns = [i * blocks + j for i in range(2) for j in range(held)]
+        matrix = jnp.concatenate([table[pl.ds(at + i * tall, tall)] for i in columns], axis=1)
+        return under(matrix, both).reshape(owners, height, LANES)
+
+    def paired(layer_of, first_of, count):
         return [
-            (l // slots, l % slots, layer_of(l), layer_of(l + 1)) for l in range(0, layers, 2)
+            (f // per, f % per * depth + z, layer_of(f, z), layer_of(f, z + 1))
+            for f in range(fields)
+            for z in (first_of + i for i in range(0, count, 2))
         ]
 
     def rim_place(f):
@@ -283,11 +338,17 @@
             return groups - 1, fields % per * depth
         return groups, f % per * depth + 2 * (f // per)
 
-    for copy in loads[2:] + fills:
-        copy.wait()
+    loads[0].wait()
+    loads[1].wait()
+    for f in range(fields):
+        for z in range(1, depth + 1):
+            y1[f, z, pl.ds(0, PAD)] = y1[f, z, pl.ds(rows, PAD)]
+            y1[f, z, pl.ds(PAD + rows, PAD)] = y1[f, z, pl.ds(PAD, PAD)]
+        for z in (0, depth + 1):
+            y4[f, z, pl.ds(PAD, rows)] = jnp.zeros((rows, cols), jnp.float32)
 
     own[...] = transform(
-        paired(lambda l: y1[l // depth, l % depth, pl.ds(PAD, rows)]), groups
+        pack(paired(lambda f, z: y1[f, z + 1, pl.ds(PAD, rows)], 0, depth), [None] * groups)
     )
     ahead_copy = pltpu.make_async_remote_copy(
         src_ref=own,
@@ -313,7 +374,10 @@
     def weigh(stage):
         return time_step / 6.0 * (1.0, 2.0, 2.0, 1.0)[stage]
 
-    def update(stage, z, r0, below, above, rim=None):
+    loads[2].wait()
+    loads[3].wait()
+
+    def update(stage, z, r0):
         state = states[stage]
         mid, xm, xp, ym, yp = [], [], [], [], []
         rolled = CHUNK + 2 * PAD
@@ -327,17 +391,17 @@
             xp.append(pltpu.roll(centre, cols - 1, 1))
         sides = [(xm, 0, 1.0, advect_xaxis), (xp, 0, -1.0, advect_xaxis)]
         sides += [(ym, 1, 1.0, advect_yaxis), (yp, 1, -1.0, advect_yaxis)]
-        for neighbour, sign in ((below, 1.0), (above, -1.0)):
-            if neighbour is not None:
-                held = [neighbour(f) for f in range(fields)]
-                sides.append((held, 2, sign, advect_zaxis))
+        here = pl.ds(pl.multiple_of(r0 + PAD, PAD), CHUNK)
+        for offset, sign in ((-1, 1.0), (1, -1.0)):
+            held = [state[f, z + offset, here] for f in range(fields)]
+            sides.append((held, 2, sign, advect_zaxis))
         factors = [
             (viscosity + sign * 0.5 * speed) + (sign * 0.5) * side[axis]
             for side, axis, sign, speed in sides
         ]
         rates = []
         for f in range(fields):
-            forcing = src[f, z, pl.ds(r0, CHUNK)]
+            forcing = src[f, z - 1, pl.ds(r0, CHUNK)]
             if f == 3:
                 total = None
                 for side, axis, sign, _ in sides:
@@ -359,11 +423,8 @@
                     total = total + push
             rates.append(total + forcing)
         share_of = weigh(stage)
-        if rim is not None:
-            for f, value in enumerate(reach(mid, 1.0 if rim else -1.0)):
-                rims[rim, f, pl.ds(r0, CHUNK)] = share_of * value
         for f in range(fields):
-            at = f * depth + z
+            at = f * depth + z - 1
             here = pl.ds(r0, CHUNK)
             begin = y1[f, z, pl.ds(pl.multiple_of(r0 + PAD, 8), CHUNK)]
             done = begin if stage == 0 else fine[at, here]
@@ -382,48 +443,73 @@
                 def _():
                     later[f, z, pl.ds(0, PAD)] = value[CHUNK - PAD :]
 
-    for stage in range(4):
+    def sweep(act):
+        def body(c, carry):
+            act(c, pl.multiple_of(c * CHUNK, CHUNK))
+            return carry
+
+        lax.fori_loop(0, chunks, body, 0)
+
+    def rim(z, r0):
+        side = jnp.where(z == depth, 1, 0)
+        sign = jnp.where(z == depth, 1.0, -1.0)
+        layer = [y4[f, z, pl.ds(pl.multiple_of(r0 + PAD, PAD), CHUNK)] for f in range(fields)]
+        for f, value in enumerate(reach(layer, sign)):
+            rims[side, f, pl.ds(r0, CHUNK)] = weigh(3) * value
+
+    early = [near_z - step * k for k in range(depth - 2)]
+    late_layers = [far_z, far_z + step]
+    early_first = jnp.where(parity == 0, 2, 0)
+    late_first = jnp.where(parity == 0, 0, depth - 2)
+
+    def settled(f, z):
+        return fine[f * depth + z]
+
+    for stage in range(3):
         state = states[stage]
 
-        def inner(i, carry):
-            z = 1 + i // chunks
-            r0 = pl.multiple_of(lax.rem(i, chunks) * CHUNK, CHUNK)
-            at = pl.ds(pl.multiple_of(r0 + PAD, 8), CHUNK)
-            update(stage, z, r0, lambda f: state[f, z - 1, at], lambda f: state[f, z + 1, at])
-            return carry
-
-        def edge(c, carry):
-            r0 = pl.multiple_of(c * CHUNK, CHUNK)
-            at = pl.ds(pl.multiple_of(r0 + PAD, 8), CHUNK)
-            for side in range(2):
-                if stage == 3:
-                    if side == 0:
-                        update(stage, 0, r0, None, lambda f: state[f, 1, at], side)
-                    else:
-                        update(stage, depth - 1, r0, lambda f: state[f, depth - 2, at], None, side)
-                    continue
-                halo_copy(stage, side, c).wait_recv()
-                here = lambda f: halo[stage, side, f, pl.ds(r0, CHUNK)]
-                if side == 0:
-                    update(stage, 0, r0, here, lambda f: state[f, 1, at])
-                else:
-                    update(stage, depth - 1, r0, lambda f: state[f, depth - 2, at], here)
-                if stage < 2:
-                    halo_copy(stage + 1, 1 - side, c).start()
-            return carry
-
-        lax.fori_loop(0, (depth - 2) * chunks, inner, 0)
-        lax.fori_loop(0, chunks, edge, 0)
+        def inner(c, r0):
+            for z in range(2, depth):
+                update(stage, z, r0)
+
+        def edge(c, r0):
+            settle(state.at[:, far_halo, span(c)], halo_recv.at[stage % 2, 1 + c])
+            update(stage, far_z, r0)
+            if stage < 2:
+                send_far(stage + 1, c)
+
+        sweep(inner)
+        settle(state.at[:, near_halo, pl.ds(PAD, rows)], halo_recv.at[stage % 2, 0])
+        sweep(lambda c, r0: update(stage, near_z, r0))
+        if stage < 2:
+            send_near(stage + 1)
+        else:
+
+            def ready(c, r0):
+                for z in early:
+                    update(3, z, r0)
+                rim(near_z, r0)
+
+            sweep(ready)
+            result = pack(paired(settled, early_first, depth - 2), [None] * groups)
+            for g in range(groups):
+                begun[g] = result[g]
+        sweep(edge)
         for level in range(levels):
             if min(level, 2) == stage:
                 heard(level)
                 if level + 1 < levels:
                     relay(level + 1)
 
-    spec = transform(
-        paired(lambda l: fine[l]) + [(*rim_place(f), rims[1, f], rims[0, f]) for f in range(fields)],
-        groups + 1,
-    )
+    def remaining(c, r0):
+        for z in late_layers:
+            update(3, z, r0)
+        rim(far_z, r0)
+
+    sweep(remaining)
+    pairs = paired(settled, late_first, 2)
+    pairs += [(*rim_place(f), rims[1, f], rims[0, f]) for f in range(fields)]
+    spec = transform(pack(pairs, [begun[g] for g in range(groups)] + [None]))
 
     def jump_copy(index, tile, target):
         return pltpu.make_async_remote_copy(
@@ -466,31 +552,22 @@
         others(lambda t, where: sent(t, where).start())
         gathered[n * spaces + s] = jumps[me]
 
-    def send_last(c, carry):
+    whole = pl.ds(PAD, rows)
+    send(y4.at[:, far_z, whole], late.at[1 - parity], 3, 1, far_to)
+    send(y4.at[:, near_z, whole], late.at[parity], 3, 0, near_to)
+
+    def finish_edge(c, r0):
+        here = pl.ds(r0, CHUNK)
         for side in range(2):
-            halo_copy(3, side, c).start()
-        return carry
-
-    def finish_edge(c, carry):
-        here = pl.ds(pl.multiple_of(c * CHUNK, CHUNK), CHUNK)
-        for side in range(2):
-            halo_copy(3, side, c).wait_recv()
-            layer = [halo[3, side, f, here] for f in range(fields)]
+            layer = [late[side, f, here] for f in range(fields)]
             for f, value in enumerate(reach(layer, -1.0 if side else 1.0)):
                 at = f * depth + side * (depth - 1)
                 fine[at, here] = fine[at, here] + weigh(3) * value
-        return carry
-
-    lax.fori_loop(0, chunks, send_last, 0)
-
-    def settle(ref, count, sem):
-        held = ref if count is None else ref.at[pl.ds(0, count)]
-        pltpu.make_async_copy(held, held, sem).wait()
 
     pl.when(n < times_n - 1)(
-        lambda: settle(gathered, (times_n - 1) * spaces - 1, jump_recv)
+        lambda: settle(gathered.at[pl.ds(0, (times_n - 1) * spaces - 1)], jump_recv)
     )
-    pl.when(n == times_n - 1)(lambda: settle(gathered, (times_n - 1) * spaces, jump_recv))
+    pl.when(n == times_n - 1)(lambda: settle(gathered.at[pl.ds(0, (times_n - 1) * spaces)], jump_recv))
 
     width = depth * spaces * keep_x
     half = depth * slot
@@ -542,7 +619,7 @@
         )
         for fp in range(per)
     ]
-    fresh = times(jnp.concatenate(lined, axis=0), zf)
+    fresh = times(jnp.concatenate(lined, axis=0), entry("zf"))
     gains = [(sym[me, fp, 0], sym[me, fp, 1]) for fp in range(per)]
     weight = jnp.where(lax.rem(lane, keep_x) == 0, 1.0, 2.0)
     zero = jnp.zeros((height, width), jnp.float32)
@@ -564,7 +641,8 @@
             size = square if size is None else size + square
         sizes_of.append(jnp.sum(size * weight, axis=0, keepdims=True))
     back = times(
-        jnp.concatenate([corrections[base + j, fp] for j in range(pair) for fp in range(per)], axis=0), zi
+        jnp.concatenate([corrections[base + j, fp] for j in range(pair) for fp in range(per)], axis=0),
+        entry("zi"),
     )
     column = jnp.sum(jnp.concatenate(sizes_of, axis=0), axis=1, keepdims=True)
     shape = (times_n, LANES)
@@ -603,8 +681,10 @@
     for dj, dk in sharers:
         mode_copy(dj, dk).start()
     modes[me] = pieces[me]
-    lax.fori_loop(0, chunks, finish_edge, 0)
-    settle(modes, owners - 1, mode_recv)
+    settle(late.at[parity], halo_recv.at[1, 1])
+    settle(late.at[1 - parity], halo_recv.at[1, 0])
+    sweep(finish_edge)
+    settle(modes.at[pl.ds(0, owners - 1)], mode_recv)
     found = modes[...].reshape(owners * height, LANES)
     total = None
     for o in range(owners):
@@ -619,27 +699,28 @@
     norms[0] = norm(jnp.where(lane == n, total, 0.0), cells)
     norms[1] = norm(total, cells * times_n)
 
-    planes = under(yi, jnp.concatenate([found, swapped(found)], axis=0))
+    planes = under_deep(entry("yi"), jnp.concatenate([found, swapped(found)], axis=0))
     for g in range(groups):
         plane = planes[g * rows : (g + 1) * rows]
         count = min(slots, layers - g * slots) // 2
         shifted = [
             plane if p == 0 else pltpu.roll(plane, LANES - 2 * p * slot, 1) for p in range(count)
         ]
-        fix = times(jnp.concatenate(shifted, axis=0), xi)
+        fix = times_deep(jnp.concatenate(shifted, axis=0), entry("xi"))
         for p in range(count):
             for i in range(2):
                 l = g * slots + 2 * p + i
                 ends[l] = fine[l] + fix[p * rows : (p + 1) * rows, i * cols : (i + 1) * cols]
 
-    pl.when(n < times_n - 1)(lambda: settle(gathered, times_n * spaces - 1, jump_send))
+    pl.when(n < times_n - 1)(lambda: settle(gathered.at[pl.ds(0, times_n * spaces - 1)], jump_send))
 
     @pl.when(n > 0)
     def _():
         ahead_copy.wait_send()
 
-    settle(halo, None, halo_send)
-    settle(modes, owners - 1, mode_send)
+    for stage in range(4):
+        settle(states[stage].at[:, pl.ds(0, 2), pl.ds(PAD, rows)], halo_send.at[stage])
+    settle(modes.at[pl.ds(0, owners - 1)], mode_send)
 
 
 def finish(ends, norms, out, slice_out, total_out, slice_held, total_held, sems):
@@ -658,19 +739,19 @@
 
     def step(starts, source):
         _, fields, depth, rows, cols = starts.shape
-        matrices, symbol = tables(fields, depth, rows, cols, times_n, spaces)
-        constants = [halves(t) for t in matrices] + [symbol]
+        places, packed, gains = tables(fields, depth, rows, cols, times_n, spaces)
+        constants = [packed, gains]
         operands = [starts, source] + [jnp.asarray(c) for c in constants]
-        _, pair, owners, _, _, height = layout(fields, depth, rows, cols, times_n, spaces)
+        groups, _, owners, _, _, height = layout(fields, depth, rows, cols, times_n, spaces)
         slot = cols // 16 * 2
         per = LANES // (slot * depth)
         chunks = rows // CHUNK
         devices = times_n * spaces
-        state = pltpu.VMEM((fields, depth, rows + 2 * PAD, cols), jnp.float32)
+        state = pltpu.VMEM((fields, depth + 2, rows + 2 * PAD, cols), jnp.float32)
         dma = pltpu.SemaphoreType.DMA
         layer_shape = (fields * depth, rows, cols)
         ends, norms = pl.pallas_call(
-            functools.partial(kernel, (times_n, spaces, fields, depth, rows, cols)),
+            functools.partial(kernel, (times_n, spaces, fields, depth, rows, cols), places),
             out_shape=(
                 pltpu.VMEM(layer_shape, jnp.float32),
                 pltpu.VMEM((2, 1, LANES), jnp.float32),
@@ -685,14 +766,15 @@
                 pltpu.VMEM((fields, depth, rows, cols), jnp.float32),
                 pltpu.VMEM(layer_shape, jnp.float32),
                 pltpu.VMEM((2, fields, rows, cols), jnp.float32),
-                pltpu.VMEM((4, 2, fields, rows, cols), jnp.float32),
+                pltpu.VMEM((2, fields, rows, cols), jnp.float32),
+                pltpu.VMEM((groups, rows, LANES), jnp.float32),
                 *[pltpu.VMEM(c.shape, c.dtype) for c in constants],
                 *[pltpu.VMEM((owners, height, LANES), jnp.float32)] * 3,
                 pltpu.VMEM((devices, height, LANES), jnp.float32),
                 pltpu.VMEM((times_n, per, height, depth * spaces * slot), jnp.float32),
                 *[pltpu.VMEM((owners, height, LANES), jnp.float32)] * 2,
-                dma((6,)), dma((len(constants),)),
-                dma, dma((2, 2, chunks)), dma((2,)), dma, dma, dma, dma,
+                dma((4,)), dma((2,)),
+                dma((4,)), dma((2, 1 + chunks)), dma((2,)), dma, dma, dma, dma,
                 pltpu.SemaphoreType.REGULAR(((times_n - 1).bit_length(), 2)),
             ],
             compiler_params=pltpu.CompilerParams(

time: 31 us -> 30 us (0.968)
  Pallas kernels: 30.2 us -> 29.2 us
    pallas_call x1, Pallas kernels: 29.4 us -> 28.3 us  [step(): pl.pallas_call(functools.partial(kernel, (times_n, spaces, fields, depth,...]
where the time goes in v5:
time: 30 us; the launch traced here: 29.9 us
  Pallas kernels  29.2 us (97%)
  between operations  0.64 us (2%)
    pallas_call x1, Pallas kernels, step(): pl.pallas_call(functools.partial(kernel, (times_n, spaces, fields, depth,...  28.3 us
    pallas_call x1, Pallas kernels, step(): pl.pallas_call(finish, out_shape=(jax.ShapeDtypeStruct(layer_shape, jnp.f...  0.88 us

profile of v5, /device:TPU:0, one launch (start us, length us, event | category | flops | bytes accessed | tf_op | source)
XLA Modules:
  0.0 29.9 jit_solution(386230941596942772)
XLA Ops:
  0.6 28.3 %shard_map.67 = (f32[20,64,128]{2,1,0:T(8,128)S(1)}, f32[2,1,128]{2,1,0:T(1,128)S(1)}) custom-call(f32[1,5,4,64,128]{4,3,2,1,0:T(8,128)} %starts.1, f32[5,4,64,128]{3,2,1,0:T(8,128)} %source.1, bf16[4416,128]{1,0:T(8,128)(2,1)} %constant.4.clone.tables_h, f32[8,2,2,8,128]{4,3,2,1,0:T(8,128)} %constant.5.clone.sym_h), custom_call_target="tpu_custom_call" | custom-call | tf_op jit(solution)/shard_map/pallas_call | solution.py:753
  29.0 0.9 %shard_map.68 = (f32[20,64,128]{2,1,0:T(8,128)}, f32[1]{0:T(128)}, f32[1]{0:T(128)}) custom-call(f32[20,64,128]{2,1,0:T(8,128)S(1)} %get-tuple-element.8.ends, f32[2,1,128]{2,1,0:T(1,128)S(1)} %get-tuple-element.9.norms), custom_call_target="tpu_custom_call" | custom-call | tf_op jit(solution)/shard_map/pallas_call | solution.py:784

commit v6 on v5

--- a/solution.py
+++ b/solution.py
@@ -173,10 +173,21 @@
     return dot(table[:, :deep], jnp.concatenate([high, low], axis=0)) + dot(table[:, deep:], high)
 
 
+def entry_of(table, places, name):
+    at, height, wide = places[name]
+    return jnp.concatenate([table[pl.ds(at + i * height, height)] for i in range(wide)], axis=1)
+
+
+def swap(values, keep_x):
+    lane = lax.broadcasted_iota(jnp.int32, (1, LANES), 1)
+    first = lax.rem(lane, 2 * keep_x) < keep_x
+    return jnp.where(first, pltpu.roll(values, LANES - keep_x, 1), -pltpu.roll(values, keep_x, 1))
+
+
 def kernel(
     sizes, places, starts, source, tables_h, sym_h,
-    ends, norms,
-    y1, y2, y3, y4, src, fine, rims, late, begun, table, sym,
+    fine, table, spectrum,
+    y1, y2, y3, y4, src, rims, late, begun, sym,
     own, jumps, ahead, gathered, corrections, pieces, modes,
     load_sem, table_sem, halo_send, halo_recv, ahead_sems, jump_send, jump_recv,
     mode_send, mode_recv, relays,
@@ -227,6 +238,8 @@
         pltpu.make_async_copy(source, src, load_sem.at[3]),
         pltpu.make_async_copy(sym_h, sym, table_sem.at[1]),
     ]
+    for copy in loads:
+        copy.start()
     for copy in edges:
         copy.wait()
     beside = jnp.where(n > 0, 1, 0) + jnp.where(n < times_n - 1, 1, 0)
@@ -286,23 +299,12 @@
 
     lax.fori_loop(0, chunks, send_first, 0)
     send_near(0)
-    for copy in loads:
-        copy.start()
     relay(0)
 
     lane = lax.broadcasted_iota(jnp.int32, (1, LANES), 1)
-    first = lax.rem(lane, slot) < keep_x
-
-    def swapped(values):
-        return jnp.where(
-            first, pltpu.roll(values, LANES - keep_x, 1), -pltpu.roll(values, keep_x, 1)
-        )
-
-    def entry(name):
-        at, height_of, wide = places[name]
-        return jnp.concatenate(
-            [table[pl.ds(at + i * height_of, height_of)] for i in range(wide)], axis=1
-        )
+    swapped = functools.partial(swap, keep_x=keep_x)
+
+    entry = functools.partial(entry_of, table, places)
 
     def pack(pairs, result):
         stacked = jnp.concatenate(
@@ -465,6 +467,12 @@
     def settled(f, z):
         return fine[f * depth + z]
 
+    def remaining(c):
+        r0 = pl.multiple_of(c * CHUNK, CHUNK)
+        for z in late_layers:
+            update(3, z, r0)
+        rim(far_z, r0)
+
     for stage in range(3):
         state = states[stage]
 
@@ -477,6 +485,8 @@
             update(stage, far_z, r0)
             if stage < 2:
                 send_far(stage + 1, c)
+            else:
+                pl.when(c >= 2)(lambda: remaining(c - 1))
 
         sweep(inner)
         settle(state.at[:, near_halo, pl.ds(PAD, rows)], halo_recv.at[stage % 2, 0])
@@ -501,12 +511,8 @@
                 if level + 1 < levels:
                     relay(level + 1)
 
-    def remaining(c, r0):
-        for z in late_layers:
-            update(3, z, r0)
-        rim(far_z, r0)
-
-    sweep(remaining)
+    remaining(chunks - 1)
+    remaining(0)
     pairs = paired(settled, late_first, 2)
     pairs += [(*rim_place(f), rims[1, f], rims[0, f]) for f in range(fields)]
     spec = transform(pack(pairs, [begun[g] for g in range(groups)] + [None]))
@@ -685,7 +691,31 @@
     settle(late.at[1 - parity], halo_recv.at[1, 0])
     sweep(finish_edge)
     settle(modes.at[pl.ds(0, owners - 1)], mode_recv)
-    found = modes[...].reshape(owners * height, LANES)
+    spectrum[...] = modes[...].reshape(owners * height, LANES)
+
+    pl.when(n < times_n - 1)(lambda: settle(gathered.at[pl.ds(0, times_n * spaces - 1)], jump_send))
+
+    @pl.when(n > 0)
+    def _():
+        ahead_copy.wait_send()
+
+    for stage in range(4):
+        settle(states[stage].at[:, pl.ds(0, 2), pl.ds(PAD, rows)], halo_send.at[stage])
+    settle(modes.at[pl.ds(0, owners - 1)], mode_send)
+
+
+def finish(
+    sizes, places, fine, table, spectrum, out, slice_out, total_out, ends, slice_held, total_held, sems
+):
+    times_n, spaces, fields, depth, rows, cols = sizes
+    keep_x = cols // 16
+    slot = 2 * keep_x
+    layers = fields * depth
+    slots = LANES // slot
+    groups, _, owners, _, used, height = layout(fields, depth, rows, cols, times_n, spaces)
+    n = lax.axis_index("tm")
+    lane = lax.broadcasted_iota(jnp.int32, (1, LANES), 1)
+    found = spectrum[...]
     total = None
     for o in range(owners):
         row = found[o * height + used : o * height + used + 1]
@@ -693,42 +723,32 @@
     cells = fields * depth * spaces * rows * cols
 
     def norm(values, count):
-        value = jnp.sqrt(jnp.sum(values, axis=1, keepdims=True) * (1.0 / count) + epsilon)
-        return jnp.broadcast_to(value, (1, LANES))
-
-    norms[0] = norm(jnp.where(lane == n, total, 0.0), cells)
-    norms[1] = norm(total, cells * times_n)
-
-    planes = under_deep(entry("yi"), jnp.concatenate([found, swapped(found)], axis=0))
+        return jnp.sqrt(jnp.sum(values, axis=1, keepdims=True) * (1.0 / count) + epsilon)
+
+    slice_held[0] = norm(jnp.where(lane == n, total, 0.0), cells)[0, 0]
+    total_held[0] = norm(total, cells * times_n)[0, 0]
+    copies = [
+        pltpu.make_async_copy(slice_held, slice_out, sems.at[0]),
+        pltpu.make_async_copy(total_held, total_out, sems.at[1]),
+    ]
+    for copy in copies:
+        copy.start()
+    planes = under_deep(
+        entry_of(table, places, "yi"), jnp.concatenate([found, swap(found, keep_x)], axis=0)
+    )
     for g in range(groups):
         plane = planes[g * rows : (g + 1) * rows]
         count = min(slots, layers - g * slots) // 2
         shifted = [
             plane if p == 0 else pltpu.roll(plane, LANES - 2 * p * slot, 1) for p in range(count)
         ]
-        fix = times_deep(jnp.concatenate(shifted, axis=0), entry("xi"))
+        fix = times_deep(jnp.concatenate(shifted, axis=0), entry_of(table, places, "xi"))
         for p in range(count):
             for i in range(2):
                 l = g * slots + 2 * p + i
                 ends[l] = fine[l] + fix[p * rows : (p + 1) * rows, i * cols : (i + 1) * cols]
-
-    pl.when(n < times_n - 1)(lambda: settle(gathered.at[pl.ds(0, times_n * spaces - 1)], jump_send))
-
-    @pl.when(n > 0)
-    def _():
-        ahead_copy.wait_send()
-
-    for stage in range(4):
-        settle(states[stage].at[:, pl.ds(0, 2), pl.ds(PAD, rows)], halo_send.at[stage])
-    settle(modes.at[pl.ds(0, owners - 1)], mode_send)
-
-
-def finish(ends, norms, out, slice_out, total_out, slice_held, total_held, sems):
-    copies = [pltpu.make_async_copy(ends, out, sems.at[0])]
-    copies[0].start()
-    for i, (held, to) in enumerate(((slice_held, slice_out), (total_held, total_out))):
-        held[0] = norms[i, 0, 0]
-        copies.append(pltpu.make_async_copy(held, to, sems.at[1 + i]))
+        held = pl.ds(g * slots, 2 * count)
+        copies.append(pltpu.make_async_copy(ends.at[held], out.at[held], sems.at[2 + g]))
         copies[-1].start()
     for copy in copies:
         copy.wait()
@@ -750,25 +770,22 @@
         state = pltpu.VMEM((fields, depth + 2, rows + 2 * PAD, cols), jnp.float32)
         dma = pltpu.SemaphoreType.DMA
         layer_shape = (fields * depth, rows, cols)
-        ends, norms = pl.pallas_call(
+        held = pl.pallas_call(
             functools.partial(kernel, (times_n, spaces, fields, depth, rows, cols), places),
             out_shape=(
                 pltpu.VMEM(layer_shape, jnp.float32),
-                pltpu.VMEM((2, 1, LANES), jnp.float32),
+                pltpu.VMEM(packed.shape, jnp.bfloat16),
+                pltpu.VMEM((owners * height, LANES), jnp.float32),
             ),
             in_specs=[pl.BlockSpec(memory_space=pltpu.HBM)] * (2 + len(constants)),
-            out_specs=(
-                pl.BlockSpec(memory_space=pltpu.VMEM),
-                pl.BlockSpec(memory_space=pltpu.VMEM),
-            ),
+            out_specs=(pl.BlockSpec(memory_space=pltpu.VMEM),) * 3,
             scratch_shapes=[
                 state, state, state, state,
                 pltpu.VMEM((fields, depth, rows, cols), jnp.float32),
-                pltpu.VMEM(layer_shape, jnp.float32),
                 pltpu.VMEM((2, fields, rows, cols), jnp.float32),
                 pltpu.VMEM((2, fields, rows, cols), jnp.float32),
                 pltpu.VMEM((groups, rows, LANES), jnp.float32),
-                *[pltpu.VMEM(c.shape, c.dtype) for c in constants],
+                pltpu.VMEM(gains.shape, jnp.float32),
                 *[pltpu.VMEM((owners, height, LANES), jnp.float32)] * 3,
                 pltpu.VMEM((devices, height, LANES), jnp.float32),
                 pltpu.VMEM((times_n, per, height, depth * spaces * slot), jnp.float32),
@@ -782,22 +799,20 @@
             ),
         )(*[pltpu.with_memory_space_constraint(a, pltpu.HBM) for a in operands])
         out, slice_norm, total_norm = pl.pallas_call(
-            finish,
+            functools.partial(finish, (times_n, spaces, fields, depth, rows, cols), places),
             out_shape=(
                 jax.ShapeDtypeStruct(layer_shape, jnp.float32),
                 jax.ShapeDtypeStruct((1,), jnp.float32),
                 jax.ShapeDtypeStruct((1,), jnp.float32),
             ),
-            in_specs=[pl.BlockSpec(memory_space=pltpu.VMEM)] * 2,
+            in_specs=[pl.BlockSpec(memory_space=pltpu.VMEM)] * 3,
             out_specs=[pl.BlockSpec(memory_space=pltpu.HBM)] * 3,
             scratch_shapes=[
-                pltpu.SMEM((1,), jnp.float32), pltpu.SMEM((1,), jnp.float32), dma((3,)),
+                pltpu.VMEM(layer_shape, jnp.float32),
+                pltpu.SMEM((1,), jnp.float32), pltpu.SMEM((1,), jnp.float32), dma((2 + groups,)),
             ],
             compiler_params=pltpu.CompilerParams(vmem_limit_bytes=VMEM_BYTES // 2),
-        )(
-            pltpu.with_memory_space_constraint(ends, pltpu.VMEM),
-            pltpu.with_memory_space_constraint(norms, pltpu.VMEM),
-        )
+        )(*[pltpu.with_memory_space_constraint(a, pltpu.VMEM) for a in held])
         return out.reshape(starts.shape), slice_norm, total_norm
 
     return jax.shard_map(

time: 30 us -> 29 us (0.967)
  Pallas kernels: 29.2 us -> 28.2 us
    pallas_call x1, Pallas kernels: 28.3 us -> 26.9 us  [step(): pl.pallas_call(functools.partial(kernel, (times_n, spaces, fields, depth,...]
    pallas_call x1, Pallas kernels: 0.88 us -> 1.39 us  [step(): pl.pallas_call(functools.partial(finish, (times_n, spaces, fields, depth,...]
where the time goes in v6:
time: 29 us; the launch traced here: 28.9 us
  Pallas kernels  28.2 us (97%)
  between operations  0.64 us (2%)
    pallas_call x1, Pallas kernels, step(): pl.pallas_call(functools.partial(kernel, (times_n, spaces, fields, depth,...  26.9 us
    pallas_call x1, Pallas kernels, step(): pl.pallas_call(functools.partial(finish, (times_n, spaces, fields, depth,...  1.39 us

profile of v6, /device:TPU:0, one launch (start us, length us, event | category | flops | bytes accessed | tf_op | source)
XLA Modules:
  0.0 28.9 jit_solution(10141685769993760789)
XLA Ops:
  0.6 26.9 %shard_map.67 = (f32[20,64,128]{2,1,0:T(8,128)S(1)}, bf16[4416,128]{1,0:T(8,128)(2,1)S(1)}, f32[64,128]{1,0:T(8,128)S(1)}) custom-call(f32[1,5,4,64,128]{4,3,2,1,0:T(8,128)} %starts.1, f32[5,4,64,128]{3,2,1,0:T(8,128)} %source.1, bf16[4416,128]{1,0:T(8,128)(2,1)} %constant.4.clone.tables_h, f32[8,2,2,8,128]{4,3,2,1,0:T(8,128)} %constant.5.clone.sym_h), custom_call_target="tpu_custom_call" | custom-call | tf_op jit(solution)/shard_map/pallas_call | solution.py:773
  27.5 1.4 %shard_map.68 = (f32[20,64,128]{2,1,0:T(8,128)}, f32[1]{0:T(128)}, f32[1]{0:T(128)}) custom-call(f32[20,64,128]{2,1,0:T(8,128)S(1)} %get-tuple-element.9.fine, bf16[4416,128]{1,0:T(8,128)(2,1)S(1)} %get-tuple-element.10.table, f32[64,128]{1,0:T(8,128)S(1)} %get-tuple-element.11.spectrum), custom_call_target="tpu_custom_call" | custom-call | tf_op jit(solution)/shard_map/pallas_call | solution.py:801

commit v7 on v6

--- a/solution.py
+++ b/solution.py
@@ -313,7 +313,8 @@
         packed = times(stacked, entry("xf"))
         result = list(result)
         for i, (g, at, _, _) in enumerate(pairs):
-            piece = packed[i * rows : (i + 1) * rows]
+            tall = packed.shape[0] // len(pairs)
+            piece = packed[i * tall : (i + 1) * tall]
             if not (isinstance(at, int) and at == 0):
                 piece = pltpu.roll(piece, at * slot, 1)
             result[g] = piece if result[g] is None else result[g] + piece
@@ -342,10 +343,14 @@
 
     loads[0].wait()
     loads[1].wait()
+    def wrap(state, z):
+        for f in range(fields):
+            state[f, z, pl.ds(0, PAD)] = state[f, z, pl.ds(rows, PAD)]
+            state[f, z, pl.ds(PAD + rows, PAD)] = state[f, z, pl.ds(PAD, PAD)]
+
+    for z in range(1, depth + 1):
+        wrap(y1, z)
     for f in range(fields):
-        for z in range(1, depth + 1):
-            y1[f, z, pl.ds(0, PAD)] = y1[f, z, pl.ds(rows, PAD)]
-            y1[f, z, pl.ds(PAD + rows, PAD)] = y1[f, z, pl.ds(PAD, PAD)]
         for z in (0, depth + 1):
             y4[f, z, pl.ds(PAD, rows)] = jnp.zeros((rows, cols), jnp.float32)
 
@@ -379,21 +384,21 @@
     loads[2].wait()
     loads[3].wait()
 
-    def update(stage, z, r0):
+    def update(stage, z, r0, size=CHUNK):
         state = states[stage]
         mid, xm, xp, ym, yp = [], [], [], [], []
-        rolled = CHUNK + 2 * PAD
+        rolled = size + 2 * PAD
         for f in range(fields):
             wide = state[f, z, pl.ds(r0, rolled)]
-            centre = wide[PAD : PAD + CHUNK]
+            centre = wide[PAD : PAD + size]
             mid.append(centre)
-            ym.append(pltpu.roll(wide, 1, 0)[PAD : PAD + CHUNK])
-            yp.append(pltpu.roll(wide, rolled - 1, 0)[PAD : PAD + CHUNK])
+            ym.append(pltpu.roll(wide, 1, 0)[PAD : PAD + size])
+            yp.append(pltpu.roll(wide, rolled - 1, 0)[PAD : PAD + size])
             xm.append(pltpu.roll(centre, 1, 1))
             xp.append(pltpu.roll(centre, cols - 1, 1))
         sides = [(xm, 0, 1.0, advect_xaxis), (xp, 0, -1.0, advect_xaxis)]
         sides += [(ym, 1, 1.0, advect_yaxis), (yp, 1, -1.0, advect_yaxis)]
-        here = pl.ds(pl.multiple_of(r0 + PAD, PAD), CHUNK)
+        here = pl.ds(pl.multiple_of(r0 + PAD, PAD), size)
         for offset, sign in ((-1, 1.0), (1, -1.0)):
             held = [state[f, z + offset, here] for f in range(fields)]
             sides.append((held, 2, sign, advect_zaxis))
@@ -403,7 +408,7 @@
         ]
         rates = []
         for f in range(fields):
-            forcing = src[f, z - 1, pl.ds(r0, CHUNK)]
+            forcing = src[f, z - 1, pl.ds(r0, size)]
             if f == 3:
                 total = None
                 for side, axis, sign, _ in sides:
@@ -427,37 +432,29 @@
         share_of = weigh(stage)
         for f in range(fields):
             at = f * depth + z - 1
-            here = pl.ds(r0, CHUNK)
-            begin = y1[f, z, pl.ds(pl.multiple_of(r0 + PAD, 8), CHUNK)]
+            here = pl.ds(r0, size)
+            begin = y1[f, z, pl.ds(pl.multiple_of(r0 + PAD, 8), size)]
             done = begin if stage == 0 else fine[at, here]
             fine[at, here] = done + share_of * rates[f]
             if stage < 3:
                 later = states[stage + 1]
                 step = (0.5, 0.5, 1.0)[stage] * time_step
                 value = begin + step * rates[f]
-                later[f, z, pl.ds(pl.multiple_of(r0 + PAD, 8), CHUNK)] = value
-
-                @pl.when(r0 == 0)
-                def _():
-                    later[f, z, pl.ds(PAD + rows, PAD)] = value[:PAD]
-
-                @pl.when(r0 == rows - CHUNK)
-                def _():
-                    later[f, z, pl.ds(0, PAD)] = value[CHUNK - PAD :]
-
-    def sweep(act):
+                later[f, z, pl.ds(pl.multiple_of(r0 + PAD, 8), size)] = value
+
+    def sweep(act, count=chunks):
         def body(c, carry):
             act(c, pl.multiple_of(c * CHUNK, CHUNK))
             return carry
 
-        lax.fori_loop(0, chunks, body, 0)
-
-    def rim(z, r0):
+        lax.fori_loop(0, count, body, 0)
+
+    def rim(z, r0, size=CHUNK):
         side = jnp.where(z == depth, 1, 0)
         sign = jnp.where(z == depth, 1.0, -1.0)
-        layer = [y4[f, z, pl.ds(pl.multiple_of(r0 + PAD, PAD), CHUNK)] for f in range(fields)]
+        layer = [y4[f, z, pl.ds(pl.multiple_of(r0 + PAD, PAD), size)] for f in range(fields)]
         for f, value in enumerate(reach(layer, sign)):
-            rims[side, f, pl.ds(r0, CHUNK)] = weigh(3) * value
+            rims[side, f, pl.ds(r0, size)] = weigh(3) * value
 
     early = [near_z - step * k for k in range(depth - 2)]
     late_layers = [far_z, far_z + step]
@@ -467,11 +464,23 @@
     def settled(f, z):
         return fine[f * depth + z]
 
-    def remaining(c):
-        r0 = pl.multiple_of(c * CHUNK, CHUNK)
+    def remaining(r0, size):
         for z in late_layers:
-            update(3, z, r0)
-        rim(far_z, r0)
+            update(3, z, r0, size)
+        rim(far_z, r0, size)
+
+    def finish_rows(spans):
+        def of(ref, *index):
+            return jnp.concatenate([ref[*index, pl.ds(r0, size)] for r0, size in spans], axis=0)
+
+        pairs = paired(lambda f, z: of(fine, f * depth + z), late_first, 2)
+        pairs += [(*rim_place(f), of(rims, 1, f), of(rims, 0, f)) for f in range(fields)]
+        result = pack(pairs, [of(begun, g) for g in range(groups)] + [None])
+        for g in range(groups + 1):
+            at = 0
+            for r0, size in spans:
+                begun[g, pl.ds(r0, size)] = result[g][at : at + size]
+                at += size
 
     for stage in range(3):
         state = states[stage]
@@ -486,11 +495,14 @@
             if stage < 2:
                 send_far(stage + 1, c)
             else:
-                pl.when(c >= 2)(lambda: remaining(c - 1))
+                pl.when(c >= 1)(lambda: remaining(pl.multiple_of(r0 - PAD, PAD), CHUNK))
 
         sweep(inner)
+        for z in range(2, depth):
+            wrap(states[stage + 1], z)
         settle(state.at[:, near_halo, pl.ds(PAD, rows)], halo_recv.at[stage % 2, 0])
         sweep(lambda c, r0: update(stage, near_z, r0))
+        wrap(states[stage + 1], near_z)
         if stage < 2:
             send_near(stage + 1)
         else:
@@ -504,18 +516,21 @@
             result = pack(paired(settled, early_first, depth - 2), [None] * groups)
             for g in range(groups):
                 begun[g] = result[g]
-        sweep(edge)
+        sweep(edge, chunks if stage < 2 else chunks - 1)
+        if stage == 2:
+            finish_rows([(PAD, rows - CHUNK - 2 * PAD)])
+            edge(chunks - 1, rows - CHUNK)
+        wrap(states[stage + 1], far_z)
         for level in range(levels):
             if min(level, 2) == stage:
                 heard(level)
                 if level + 1 < levels:
                     relay(level + 1)
 
-    remaining(chunks - 1)
-    remaining(0)
-    pairs = paired(settled, late_first, 2)
-    pairs += [(*rim_place(f), rims[1, f], rims[0, f]) for f in range(fields)]
-    spec = transform(pack(pairs, [begun[g] for g in range(groups)] + [None]))
+    remaining(rows - PAD, PAD)
+    remaining(0, PAD)
+    finish_rows([(rows - CHUNK - PAD, CHUNK + PAD), (0, PAD)])
+    spec = transform([begun[g] for g in range(groups + 1)])
 
     def jump_copy(index, tile, target):
         return pltpu.make_async_remote_copy(
@@ -784,7 +799,7 @@
                 pltpu.VMEM((fields, depth, rows, cols), jnp.float32),
                 pltpu.VMEM((2, fields, rows, cols), jnp.float32),
                 pltpu.VMEM((2, fields, rows, cols), jnp.float32),
-                pltpu.VMEM((groups, rows, LANES), jnp.float32),
+                pltpu.VMEM((groups + 1, rows, LANES), jnp.float32),
                 pltpu.VMEM(gains.shape, jnp.float32),
                 *[pltpu.VMEM((owners, height, LANES), jnp.float32)] * 3,
                 pltpu.VMEM((devices, height, LANES), jnp.float32),

time: 29 us -> 28.9 us (level)
  no operation moved by 1% of the time
where the time goes in v7:
time: 28.9 us; the launch traced here: 28.8 us
  Pallas kernels  28.1 us (97%)
  between operations  0.64 us (2%)
    pallas_call x1, Pallas kernels, step(): pl.pallas_call(functools.partial(kernel, (times_n, spaces, fields, depth,...  26.7 us
    pallas_call x1, Pallas kernels, step(): pl.pallas_call(functools.partial(finish, (times_n, spaces, fields, depth,...  1.39 us

profile of v7, /device:TPU:0, one launch (start us, length us, event | category | flops | bytes accessed | tf_op | source)
XLA Modules:
  0.0 28.8 jit_solution(2345409395250039760)
XLA Ops:
  0.6 26.7 %shard_map.67 = (f32[20,64,128]{2,1,0:T(8,128)S(1)}, bf16[4416,128]{1,0:T(8,128)(2,1)S(1)}, f32[64,128]{1,0:T(8,128)S(1)}) custom-call(f32[1,5,4,64,128]{4,3,2,1,0:T(8,128)} %starts.1, f32[5,4,64,128]{3,2,1,0:T(8,128)} %source.1, bf16[4416,128]{1,0:T(8,128)(2,1)} %constant.4.clone.tables_h, f32[8,2,2,8,128]{4,3,2,1,0:T(8,128)} %constant.5.clone.sym_h), custom_call_target="tpu_custom_call" | custom-call | tf_op jit(solution)/shard_map/pallas_call | solution.py:788
  27.4 1.4 %shard_map.68 = (f32[20,64,128]{2,1,0:T(8,128)}, f32[1]{0:T(128)}, f32[1]{0:T(128)}) custom-call(f32[20,64,128]{2,1,0:T(8,128)S(1)} %get-tuple-element.9.fine, bf16[4416,128]{1,0:T(8,128)(2,1)S(1)} %get-tuple-element.10.table, f32[64,128]{1,0:T(8,128)S(1)} %get-tuple-element.11.spectrum), custom_call_target="tpu_custom_call" | custom-call | tf_op jit(solution)/shard_map/pallas_call | solution.py:816

commit v8 on v7

--- a/solution.py
+++ b/solution.py
@@ -149,7 +149,9 @@
     high, low = split(values)
     wide = table.shape[1] // 2
     if wide > LANES:
-        return dot(high, table[:, :wide]) + dot(low, table[:, :wide]) + dot(high, table[:, wide:])
+        stacked = dot(jnp.concatenate([high, low], axis=0), table[:, :wide])
+        tall = values.shape[0]
+        return stacked[:tall] + stacked[tall:] + dot(high, table[:, wide:])
     both = dot(high, table)
     return both[:, :wide] + dot(low, table[:, :wide]) + both[:, wide:]
 
@@ -740,14 +742,7 @@
     def norm(values, count):
         return jnp.sqrt(jnp.sum(values, axis=1, keepdims=True) * (1.0 / count) + epsilon)
 
-    slice_held[0] = norm(jnp.where(lane == n, total, 0.0), cells)[0, 0]
-    total_held[0] = norm(total, cells * times_n)[0, 0]
-    copies = [
-        pltpu.make_async_copy(slice_held, slice_out, sems.at[0]),
-        pltpu.make_async_copy(total_held, total_out, sems.at[1]),
-    ]
-    for copy in copies:
-        copy.start()
+    copies = []
     planes = under_deep(
         entry_of(table, places, "yi"), jnp.concatenate([found, swap(found, keep_x)], axis=0)
     )
@@ -765,6 +760,16 @@
         held = pl.ds(g * slots, 2 * count)
         copies.append(pltpu.make_async_copy(ends.at[held], out.at[held], sems.at[2 + g]))
         copies[-1].start()
+        if g == 0:
+            slice_held[0] = norm(jnp.where(lane == n, total, 0.0), cells)[0, 0]
+            total_held[0] = norm(total, cells * times_n)[0, 0]
+            small = [
+                pltpu.make_async_copy(slice_held, slice_out, sems.at[0]),
+                pltpu.make_async_copy(total_held, total_out, sems.at[1]),
+            ]
+            for copy in small:
+                copy.start()
+            copies += small
     for copy in copies:
         copy.wait()
 

time: 28.9 us -> 28.9 us (level)
  no operation moved by 1% of the time
where the time goes in v8:
time: 28.9 us; the launch traced here: 28.7 us
  Pallas kernels  28.1 us (97%)
  between operations  0.64 us (2%)
    pallas_call x1, Pallas kernels, step(): pl.pallas_call(functools.partial(kernel, (times_n, spaces, fields, depth,...  26.7 us
    pallas_call x1, Pallas kernels, step(): pl.pallas_call(functools.partial(finish, (times_n, spaces, fields, depth,...  1.39 us

profile of v8, /device:TPU:0, one launch (start us, length us, event | category | flops | bytes accessed | tf_op | source)
XLA Modules:
  0.0 28.7 jit_solution(12141265298845149476)
XLA Ops:
  0.6 26.7 %shard_map.67 = (f32[20,64,128]{2,1,0:T(8,128)S(1)}, bf16[4416,128]{1,0:T(8,128)(2,1)S(1)}, f32[64,128]{1,0:T(8,128)S(1)}) custom-call(f32[1,5,4,64,128]{4,3,2,1,0:T(8,128)} %starts.1, f32[5,4,64,128]{3,2,1,0:T(8,128)} %source.1, bf16[4416,128]{1,0:T(8,128)(2,1)} %constant.4.clone.tables_h, f32[8,2,2,8,128]{4,3,2,1,0:T(8,128)} %constant.5.clone.sym_h), custom_call_target="tpu_custom_call" | custom-call | tf_op jit(solution)/shard_map/pallas_call | solution.py:793
  27.3 1.4 %shard_map.68 = (f32[20,64,128]{2,1,0:T(8,128)}, f32[1]{0:T(128)}, f32[1]{0:T(128)}) custom-call(f32[20,64,128]{2,1,0:T(8,128)S(1)} %get-tuple-element.9.fine, bf16[4416,128]{1,0:T(8,128)(2,1)S(1)} %get-tuple-element.10.table, f32[64,128]{1,0:T(8,128)S(1)} %get-tuple-element.11.spectrum), custom_call_target="tpu_custom_call" | custom-call | tf_op jit(solution)/shard_map/pallas_call | solution.py:821

commit v9 on v8

--- a/solution.py
+++ b/solution.py
@@ -221,7 +221,8 @@
 
     for offset in range(1, spaces):
         enter(n, lax.rem(s + offset, spaces))
-    near(1, lambda side, target: enter(target, s))
+    enter(n + 1 - 2 * lax.rem(n, 2), s)
+    near(2, lambda side, target: enter(target, s))
     edges = [
         pltpu.make_async_copy(
             starts.at[0, :, z], y1.at[:, z + 1, pl.ds(PAD, rows)], load_sem.at[min(z, 1)]
@@ -244,8 +245,8 @@
         copy.start()
     for copy in edges:
         copy.wait()
-    beside = jnp.where(n > 0, 1, 0) + jnp.where(n < times_n - 1, 1, 0)
-    pl.semaphore_wait(barrier, spaces - 1 + beside)
+    beside = jnp.where(n > 1, 1, 0) + jnp.where(n < times_n - 2, 1, 0)
+    pl.semaphore_wait(barrier, spaces + beside)
 
     def relay(level):
         near(
@@ -253,6 +254,11 @@
             lambda side, target: pl.semaphore_signal(
                 relays.at[level, side], inc=1, device_id=(target, s), device_id_type=MESH
             ),
+        )
+
+    def greet():
+        pl.semaphore_signal(
+            relays.at[0, 0], inc=1, device_id=(n + 1 - 2 * lax.rem(n, 2), s), device_id_type=MESH
         )
 
     def heard(level):
@@ -301,7 +307,7 @@
 
     lax.fori_loop(0, chunks, send_first, 0)
     send_near(0)
-    relay(0)
+    greet()
 
     lane = lax.broadcasted_iota(jnp.int32, (1, LANES), 1)
     swapped = functools.partial(swap, keep_x=keep_x)
@@ -368,9 +374,6 @@
         device_id_type=MESH,
     )
 
-    @pl.when(n > 0)
-    def _():
-        ahead_copy.start()
 
     shift = viscosity - diffusivity
 
@@ -525,9 +528,14 @@
         wrap(states[stage + 1], far_z)
         for level in range(levels):
             if min(level, 2) == stage:
-                heard(level)
+                if level == 0:
+                    pl.semaphore_wait(relays.at[0, 0], 1)
+                else:
+                    heard(level)
                 if level + 1 < levels:
                     relay(level + 1)
+        if stage == 1:
+            pl.when(n > 0)(lambda: ahead_copy.start())
 
     remaining(rows - PAD, PAD)
     remaining(0, PAD)

time: 28.9 us -> 28.9 us (level)
  no operation moved by 1% of the time
where the time goes in v9:
time: 28.9 us; the launch traced here: 28.7 us
  Pallas kernels  28.1 us (97%)
  between operations  0.64 us (2%)
    pallas_call x1, Pallas kernels, step(): pl.pallas_call(functools.partial(kernel, (times_n, spaces, fields, depth,...  26.7 us
    pallas_call x1, Pallas kernels, step(): pl.pallas_call(functools.partial(finish, (times_n, spaces, fields, depth,...  1.4 us

profile of v9, /device:TPU:0, one launch (start us, length us, event | category | flops | bytes accessed | tf_op | source)
XLA Modules:
  0.0 28.7 jit_solution(1751366781371736861)
XLA Ops:
  0.6 26.7 %shard_map.67 = (f32[20,64,128]{2,1,0:T(8,128)S(1)}, bf16[4416,128]{1,0:T(8,128)(2,1)S(1)}, f32[64,128]{1,0:T(8,128)S(1)}) custom-call(f32[1,5,4,64,128]{4,3,2,1,0:T(8,128)} %starts.1, f32[5,4,64,128]{3,2,1,0:T(8,128)} %source.1, bf16[4416,128]{1,0:T(8,128)(2,1)} %constant.4.clone.tables_h, f32[8,2,2,8,128]{4,3,2,1,0:T(8,128)} %constant.5.clone.sym_h), custom_call_target="tpu_custom_call" | custom-call | tf_op jit(solution)/shard_map/pallas_call | solution.py:801
  27.3 1.4 %shard_map.68 = (f32[20,64,128]{2,1,0:T(8,128)}, f32[1]{0:T(128)}, f32[1]{0:T(128)}) custom-call(f32[20,64,128]{2,1,0:T(8,128)S(1)} %get-tuple-element.9.fine, bf16[4416,128]{1,0:T(8,128)(2,1)S(1)} %get-tuple-element.10.table, f32[64,128]{1,0:T(8,128)S(1)} %get-tuple-element.11.spectrum), custom_call_target="tpu_custom_call" | custom-call | tf_op jit(solution)/shard_map/pallas_call | solution.py:829

commit v10 on v9

--- a/solution.py
+++ b/solution.py
@@ -521,7 +521,8 @@
             result = pack(paired(settled, early_first, depth - 2), [None] * groups)
             for g in range(groups):
                 begun[g] = result[g]
-        sweep(edge, chunks if stage < 2 else chunks - 1)
+        for c in range(chunks if stage < 2 else chunks - 1):
+            edge(c, c * CHUNK)
         if stage == 2:
             finish_rows([(PAD, rows - CHUNK - 2 * PAD)])
             edge(chunks - 1, rows - CHUNK)

time: 28.9 us -> 28.9 us (level)
  no operation moved by 1% of the time
where the time goes in v10:
time: 28.9 us; the launch traced here: 28.7 us
  Pallas kernels  28.1 us (97%)
  between operations  0.64 us (2%)
    pallas_call x1, Pallas kernels, step(): pl.pallas_call(functools.partial(kernel, (times_n, spaces, fields, depth,...  26.7 us
    pallas_call x1, Pallas kernels, step(): pl.pallas_call(functools.partial(finish, (times_n, spaces, fields, depth,...  1.4 us

profile of v10, /device:TPU:0, one launch (start us, length us, event | category | flops | bytes accessed | tf_op | source)
XLA Modules:
  0.0 28.7 jit_solution(567159326517786705)
XLA Ops:
  0.6 26.7 %shard_map.67 = (f32[20,64,128]{2,1,0:T(8,128)S(1)}, bf16[4416,128]{1,0:T(8,128)(2,1)S(1)}, f32[64,128]{1,0:T(8,128)S(1)}) custom-call(f32[1,5,4,64,128]{4,3,2,1,0:T(8,128)} %starts.1, f32[5,4,64,128]{3,2,1,0:T(8,128)} %source.1, bf16[4416,128]{1,0:T(8,128)(2,1)} %constant.4.clone.tables_h, f32[8,2,2,8,128]{4,3,2,1,0:T(8,128)} %constant.5.clone.sym_h), custom_call_target="tpu_custom_call" | custom-call | tf_op jit(solution)/shard_map/pallas_call | solution.py:802
  27.3 1.4 %shard_map.68 = (f32[20,64,128]{2,1,0:T(8,128)}, f32[1]{0:T(128)}, f32[1]{0:T(128)}) custom-call(f32[20,64,128]{2,1,0:T(8,128)S(1)} %get-tuple-element.9.fine, bf16[4416,128]{1,0:T(8,128)(2,1)S(1)} %get-tuple-element.10.table, f32[64,128]{1,0:T(8,128)S(1)} %get-tuple-element.11.spectrum), custom_call_target="tpu_custom_call" | custom-call | tf_op jit(solution)/shard_map/pallas_call | solution.py:830
